TPU v7x, 32 devices: a whole 2x2x4 slice. The times are simulated.
32 devices in a mesh: groups: 2 (over y), section: 4 (over z), tp: 2 (over core), sp: 2 (over x).
Axes of the slice: x: 2, y: 2, z: 4, core: 2. Of those that a mesh axis runs over, the one named last changes fastest.
Arguments:
- hidden: bfloat16 [1024, 6144], P(('groups', 'sp', 'section'), 'tp'), parts along dimension 0, may hold values from -6 to 6
- modulation: float32 [2, 6144], P(None, 'tp'), may hold values from -2 to 2
- time_embed: float32 [12288], P(('groups', 'tp')), parts along dimension 0, may hold values from -2 to 2
- head_weight: bfloat16 [6144, 64], P('tp'), may hold values from -0.078125 to 0.078125
- head_bias: float32 [64], replicated, may hold values from -2 to 2
- noisy: bfloat16 [16, 16, 16, 16], P(('groups', 'sp'), None, 'section'), parts along dimension 0, may hold values from -6 to 6
- step_size: float32 [2], P('groups'), parts along dimension 0, may hold values from 0.2 to 0.6
- latent_mean: float32 [16], replicated, may hold values from -2 to 2
- latent_std: float32 [16], replicated, may hold values from 0.5 to 2
- in_weight: bfloat16 [27, 16, 512], P(None, None, 'tp'), may hold values from -0.3125 to 0.3125
- in_bias: float32 [512], P('tp'), may hold values from -2 to 2
- norm_gain: float32 [512], replicated, may hold values from 0.25 to 1.75
- conv_weight: bfloat16 [27, 512, 512], P(None, 'section', 'tp'), may hold values from -0.0546875 to 0.0546875
- conv_bias: float32 [512], P('tp'), may hold values from -2 to 2
Outputs:
- decoded: bfloat16 [16, 16, 16, 512], P(('groups', 'sp'), None, 'section', 'tp'), parts along dimension 0
There are 2 independent parts, one for each index of `groups`. A program takes and returns all parts, laid end to end along the dimension named above; an argument that names none is the same for every part. Nothing has to cross between parts.
All inputs are finite; a program needn't handle non-finite values.
Results may differ from a plain program's by a relative error of at most 0.006.
Values may be sent and summed in bfloat16 or wider, within the bound.
A program may use at most 128 MiB of HBM per device.

v0:
```python
import functools

import jax
import jax.numpy as jnp
from jax import lax
from jax.experimental import pallas as pl
from jax.experimental.pallas import tpu as pltpu
from jax.sharding import PartitionSpec as P

D = 6144


def padded_2(value, sides, width):
    for axis, dim in sides:
        count, length = (lax.axis_size(axis), value.shape[dim])
        up = [(i, (i + 1) % count) for i in range(count - 1)]
        down = [(j, i) for i, j in up]
        last = lax.slice_in_dim(value, length - width, length, axis=dim)
        leading = lax.slice_in_dim(value, 0, width, axis=dim)
        before = lax.ppermute(last, axis, up)
        after = lax.ppermute(leading, axis, down)
        value = jnp.concatenate([before, value, after], axis=dim)
    return value


def passed_along(value, axis, by):
    count = lax.axis_size(axis)
    pairs = [(i, i + by) for i in range(count) if 0 <= i + by < count]
    return lax.ppermute(value, axis, pairs)


def conv_taps(padded, weight, frames, height, columns):
    channels = padded.shape[3]
    result = jnp.zeros((frames * height * columns, weight.shape[2]), jnp.float32)
    for offset_time in range(3):
        for offset_row in range(3):
            slab = padded[offset_time : offset_time + frames, offset_row : offset_row + height]
            window = jnp.concatenate(
                [slab[:, :, 0:columns], slab[:, :, 1 : columns + 1], slab[:, :, 2 : columns + 2]],
                axis=3,
            )
            first = 9 * offset_time + 3 * offset_row
            taps = weight[first : first + 3].reshape(3 * channels, weight.shape[2])
            result = result + jnp.dot(
                window.reshape(-1, 3 * channels), taps, preferred_element_type=jnp.float32
            )
    return result


def activate(source, gain_vector):
    values = source.astype(jnp.float32)
    squares = jnp.mean(values * values, axis=-1, keepdims=True)
    return jax.nn.silu(values * lax.rsqrt(squares + 1e-06) * gain_vector).astype(jnp.bfloat16)


def pad_rows(source):
    return jnp.pad(source, ((0, 0), (1, 1), (0, 0), (0, 0)))


def shards(
    hidden,
    modulation,
    time_embed,
    head_weight,
    head_bias,
    noisy,
    step_size,
    latent_mean,
    latent_std,
    in_weight,
    in_bias,
    norm_gain,
    conv_weight,
    conv_bias,
):
    frames, height, columns, lat_channels = noisy.shape
    sections = lax.axis_size("section")
    half_channels = in_weight.shape[2]
    values = hidden.astype(jnp.float32)
    row_sums, square_sums = lax.psum(
        (jnp.sum(values, axis=1), jnp.sum(values * values, axis=1)), "tp"
    )
    average = row_sums / D
    variance = square_sums / D - average * average
    shift_term = modulation[0] + time_embed
    scale_term = modulation[1] + time_embed
    modulated = (
        (values - average[:, None]) * lax.rsqrt(variance[:, None] + 1e-06) * (1.0 + scale_term)
        + shift_term
    ).astype(jnp.bfloat16)
    partial_sum = jnp.dot(modulated, head_weight, preferred_element_type=jnp.float32)
    velocity = (lax.psum(partial_sum, "tp") + head_bias).astype(jnp.bfloat16)
    band_rows = velocity.shape[0] * 2 // (columns * sections)
    outgoing = velocity.reshape(band_rows, sections, -1)
    arrived = lax.all_to_all(outgoing, "section", split_axis=1, concat_axis=0, tiled=True)
    latent_field = arrived.reshape(frames, height // 2, columns // 2, 2, 2, lat_channels)
    latent_field = jnp.transpose(latent_field, (0, 1, 3, 2, 4, 5)).reshape(
        frames, height, columns, lat_channels
    )
    latent = (
        (noisy.astype(jnp.float32) - step_size[0] * latent_field.astype(jnp.float32)) * latent_std
        + latent_mean
    ).astype(jnp.bfloat16)
    latent_wide = padded_2(latent, (("section", 2),), 2)
    earlier = passed_along(latent_wide, "sp", 1)
    stacked = pad_rows(jnp.concatenate([earlier, latent_wide], axis=0))
    extended = (conv_taps(stacked, in_weight, frames + 2, height, columns + 2) + in_bias).astype(
        jnp.bfloat16
    )
    extended = extended.reshape(frames + 2, height, columns + 2, half_channels)
    upblock_half = extended[2:, :, 1 : columns + 1]
    extended_full = lax.all_gather(extended, "tp", axis=3, tiled=True)
    normed = activate(extended_full, norm_gain)
    frame_index = lax.axis_index("sp") * frames - 2 + jnp.arange(frames + 2, dtype=jnp.int32)
    column_index = (
        lax.axis_index("section") * columns - 1 + jnp.arange(columns + 2, dtype=jnp.int32)
    )
    inside_cols = (column_index >= 0) & (column_index < columns * sections)
    inside = (frame_index >= 0)[:, None, None, None] & inside_cols[None, None, :, None]
    conv_input = pad_rows(jnp.where(inside, normed, jnp.zeros_like(normed)))
    full_weight = lax.all_gather(conv_weight, "section", axis=1, tiled=True)
    mixed = conv_taps(conv_input, full_weight, frames, height, columns)
    decoded = (
        upblock_half.astype(jnp.float32).reshape(-1, half_channels) + mixed + conv_bias
    ).astype(jnp.bfloat16)
    return decoded.reshape(frames, height, columns, half_channels)


def iota(shape, dim):
    return lax.broadcasted_iota(jnp.int32, shape, dim)


def dot(left, right):
    return jnp.dot(left, right, preferred_element_type=jnp.float32)


def dot_rows(left, right):
    return lax.dot_general(
        left, right, (((1,), (1,)), ((), ())), preferred_element_type=jnp.float32
    )


def pieces(value):
    high = value.astype(jnp.bfloat16)
    rest = value - high.astype(jnp.float32)
    middle = rest.astype(jnp.bfloat16)
    low = (rest - middle.astype(jnp.float32)).astype(jnp.bfloat16)
    return high.astype(jnp.float32), middle.astype(jnp.float32), low.astype(jnp.float32)


def block_kernel(
    sizes,
    modulation,
    time_embed,
    head_bias,
    noisy,
    step_size,
    latent_std,
    latent_mean,
    in_bias,
    norm_gain,
    conv_bias,
    hidden_far,
    head_far,
    in_far,
    conv_far,
    out,
    hidden,
    head_weight,
    in_weight,
    part_a,
    part_s,
    part_w,
    peer_a,
    peer_s,
    peer_w,
    peer_weight,
    peer_bias,
    fields,
    noises,
    noise_own,
    expanded,
    stacked,
    taps_in,
    ups,
    wide,
    weight,
    send_buf,
    recv_buf,
    final,
    load_sems,
    pair_send,
    pair_recv,
    noise_send,
    noise_recv,
    field_send,
    field_recv,
    sum_send,
    sum_recv,
):
    sections, clips_sp, frames, height, columns, lat, channels = sizes
    rows_i, cols_j = height // 2, columns * sections // 2
    width = columns * sections
    tokens = rows_i * cols_j
    near = frames + 2
    half = in_weight.shape[2]
    sec, core, spi = lax.axis_index("section"), lax.axis_index("tp"), lax.axis_index("sp")
    nxt, prv = lax.rem(spi + 1, clips_sp), lax.rem(spi + clips_sp - 1, clips_sp)
    peer = {"tp": 1 - core}

    loads = [
        pltpu.make_async_copy(source, target, load_sems.at[n])
        for n, (source, target) in enumerate(
            ((hidden_far, hidden), (head_far, head_weight), (in_far, in_weight), (conv_far, weight))
        )
    ]
    for c in loads:
        c.start()
    barrier = pltpu.get_barrier_semaphore()
    pl.semaphore_signal(barrier, inc=1, device_id=peer)
    for k in range(1, sections):
        pl.semaphore_signal(barrier, inc=1, device_id={"section": lax.rem(sec + k, sections)})
    for k in range(sections):
        pl.semaphore_signal(
            barrier, inc=1, device_id={"section": lax.rem(sec + k, sections), "sp": prv}
        )

    def pair_copy(n, source, target):
        return pltpu.make_async_remote_copy(
            source, target, pair_send.at[n], pair_recv.at[n], device_id=peer
        )

    def spread(source, target, send, recv):
        made = []
        for k in range(1, sections):
            made.append(
                pltpu.make_async_remote_copy(
                    source, target.at[0, k], send.at[0, k], recv.at[0, k],
                    device_id={"section": lax.rem(sec + k, sections)},
                )
            )
        for k in range(sections):
            made.append(
                pltpu.make_async_remote_copy(
                    source, target.at[1, k], send.at[1, k], recv.at[1, k],
                    device_id={"section": lax.rem(sec + k, sections), "sp": nxt},
                )
            )
        return made

    lanes = 4 * lat
    tile = rows_i * columns // 2
    share = frames * tile
    to, at = iota((4 * share, 4 * share), 0), iota((4 * share, 4 * share), 1)
    cell, token = lax.div(to, share), lax.rem(to, share)
    line_f = lax.div(token, tile)
    jl, line_i = lax.div(lax.rem(token, tile), rows_i), line_f * rows_i + lax.rem(token, rows_i)
    home = (2 * line_i + lax.div(cell, 2)) * columns + 2 * jl + lax.rem(cell, 2)
    moved = dot((home == at).astype(jnp.bfloat16), noisy[...]).astype(jnp.bfloat16)
    src, dst = iota((lat, lanes), 0), iota((lat, lanes), 1)
    own_noise = jnp.zeros((share, lanes), jnp.float32)
    for n in range(4):
        own_noise = own_noise + dot(
            moved[n * share : (n + 1) * share], (src + n * lat == dst).astype(jnp.bfloat16)
        )
    noise_own[...] = own_noise.astype(jnp.bfloat16).reshape(noise_own.shape)

    features = hidden.shape[1]
    scale = 1.0 + (modulation[1:2, :] + time_embed[...])
    shift = modulation[0:1, :] + time_embed[...]
    loads[0].wait()
    values = hidden[...].astype(jnp.float32)
    own_sum = jnp.sum(values, axis=1, keepdims=True)
    own_square = jnp.sum(values * values, axis=1, keepdims=True)
    center = own_sum / features
    centred = ((values - center) * scale).astype(jnp.bfloat16)
    loads[1].wait()
    part_a[...] = dot_rows(centred, head_weight[...])
    part_s[...] = jnp.where(iota(part_s.shape, 1) < part_s.shape[1] // 2, own_sum, own_square)
    row = iota((8, features), 0)
    lines = jnp.zeros((8, features), jnp.float32)
    for n, piece in enumerate(pieces(scale) + pieces(shift)):
        lines = jnp.where(row == n, piece, lines)
    made = dot_rows(lines.astype(jnp.bfloat16), head_weight[...])
    line = iota(made.shape, 0)
    own_scale = jnp.sum(jnp.where(line < 3, made, 0.0), axis=0, keepdims=True)
    own_shift = jnp.sum(jnp.where(line >= 3, made, 0.0), axis=0, keepdims=True)
    part_w[...] = jnp.where(line == 0, own_scale, own_shift)
    pair = [
        pair_copy(2, part_a, peer_a), pair_copy(3, part_s, peer_s), pair_copy(4, part_w, peer_w)
    ]
    loads[2].wait()
    early = [pair_copy(0, in_weight, peer_weight), pair_copy(1, in_bias, peer_bias)]
    noise_copies = []
    for k in range(1, sections):
        d = lax.rem(sec + k, sections)
        noise_copies.append(
            pltpu.make_async_remote_copy(
                noise_own.at[d], noises.at[k], noise_send.at[k], noise_recv.at[k],
                device_id={"section": d},
            )
        )
    pl.semaphore_wait(barrier, 2 * sections)
    for c in pair + noise_copies + early:
        c.start()
    for c in pair:
        c.wait()
    far_sum = peer_s[:, 0:1]
    far_square = peer_s[:, part_s.shape[1] // 2 : part_s.shape[1] // 2 + 1]
    average = (own_sum + far_sum) / D
    variance = (own_square + far_square) / D - average * average
    body = (
        part_a[...]
        + peer_a[...]
        - (average - center) * own_scale
        - (average - far_sum / features) * peer_w[0:1, :]
    )
    velocity = (
        lax.rsqrt(variance + 1e-06) * body + (own_shift + peer_w[1:2, :]) + head_bias[...]
    ).astype(jnp.bfloat16)
    to, at = iota((tokens, tokens), 0), iota((tokens, tokens), 1)
    swap = (lax.rem(to, rows_i) * cols_j + lax.div(to, rows_i) == at).astype(jnp.bfloat16)
    field = dot(swap, velocity)
    for c in noise_copies:
        c.wait()
    noises[0] = noise_own[sec]
    noise = jnp.concatenate(
        [noises[lax.rem(sec + sections - g, sections)] for g in range(sections)], axis=0
    ).astype(jnp.float32)
    std = jnp.concatenate([latent_std[...]] * 4, axis=1)
    mean_latent = jnp.concatenate([latent_mean[...]] * 4, axis=1)
    latent = (noise - step_size[0] * field) * std + mean_latent
    folded = tokens // 2
    fields[0, 0] = jnp.concatenate([latent[:folded], latent[folded:]], axis=1).astype(jnp.bfloat16)
    field_copies = spread(fields.at[0, 0], fields, field_send, field_recv)
    for c in field_copies:
        c.start()

    for c in early:
        c.wait()
    taps_in[...] = jnp.zeros_like(taps_in)
    line_size = 4 * 2 * lat
    for q in range(2):
        for e in range(3):
            col = q + e
            step_j, odd = (col + 1) // 2 - q, (col + 1) % 2
            for a in range(3):
                for b in range(3):
                    tap = 9 * a + 3 * b + e
                    for p in range(2):
                        first = step_j * 3 * line_size + a * line_size + (p + b) * 2 * lat + odd * lat
                        left = p * 2 * half
                        taps_in[q, first : first + lat, left : left + half] = in_weight[tap]
                        taps_in[q, first : first + lat, left + half : left + 2 * half] = peer_weight[tap]
    expanded[...] = jnp.zeros_like(expanded)
    wide[0] = jnp.zeros_like(wide[0])
    wide[width + 1] = jnp.zeros_like(wide[0])
    for c in field_copies:
        c.wait()

    shape = (2 * lanes, 2 * line_size)
    src, dst = iota(shape, 0), iota(shape, 1)
    same = lax.div(src, lanes) == lax.div(dst, line_size)
    src, dst = lax.rem(src, lanes), lax.rem(dst, line_size)
    place_mid = (same & (src + 2 * lat == dst)).astype(jnp.bfloat16)
    place_before = (same & (src == dst + 2 * lat) & (dst < 2 * lat)).astype(jnp.bfloat16)
    place_after = (same & (src + 6 * lat == dst) & (dst >= 6 * lat)).astype(jnp.bfloat16)
    lines_f = jnp.concatenate(
        [
            fields[slot, lax.rem(sec + sections - f, sections)]
            for slot in (1, 0)
            for f in range(frames)
        ],
        axis=0,
    ).astype(jnp.float32)
    count = 2 * frames * folded
    f_row = iota((count, 2 * lanes), 0)
    i_row = lax.rem(f_row, rows_i)
    lines_f = jnp.where((f_row >= frames * folded) | (spi > 0), lines_f, 0.0)
    before = jnp.where(i_row == 0, 0.0, pltpu.roll(lines_f, 1, 0))
    after = jnp.where(i_row == rows_i - 1, 0.0, pltpu.roll(lines_f, count - 1, 0))
    line_values = (
        dot(before.astype(jnp.bfloat16), place_before)
        + dot(lines_f.astype(jnp.bfloat16), place_mid)
        + dot(after.astype(jnp.bfloat16), place_after)
    )
    half_j = cols_j // 2
    for f in range(2 * frames):
        for side in range(2):
            expanded[1 + side * half_j : 1 + (side + 1) * half_j, f] = line_values[
                f * folded : (f + 1) * folded, side * line_size : (side + 1) * line_size
            ].reshape(half_j, rows_i, line_size)
    block = near * rows_i
    for j in range(cols_j + 2):
        for a in range(3):
            stacked[j * block : (j + 1) * block, a * line_size : (a + 1) * line_size] = (
                expanded[j, a : a + near].reshape(block, line_size).astype(jnp.bfloat16)
            )
    parts = half // channels
    tall = near * height
    for q in range(2):
        lhs = jnp.concatenate(
            [
                stacked[q * block : (q + cols_j) * block, :],
                stacked[(q + 1) * block : (q + 1 + cols_j) * block, :],
            ],
            axis=1,
        )
        for p in range(2):
            for h in range(2):
                left = (p * 2 + h) * half
                bias = in_bias[...] if h == 0 else peer_bias[...]
                up = dot(lhs, taps_in[q, :, left : left + half]) + bias
                up = up.astype(jnp.bfloat16).astype(jnp.float32)
                for j in range(cols_j):
                    for n in range(parts):
                        ups[
                            h * parts + n, pl.ds((2 * j + q) * tall + p, block, stride=2), :
                        ] = up[j * block : (j + 1) * block, n * channels : (n + 1) * channels]

    mine = lax.rem(sec + parts * core, 2 * parts)
    gain = norm_gain[pl.ds(sec, 1), :]
    h_row = lax.rem(iota((tall, channels), 0), height)
    valid = (spi > 0) | (iota((tall, channels), 0) >= 2 * height)

    def normalise(w, carry):
        at_w = pl.ds(pl.multiple_of(w * tall, tall), tall)
        squares = jnp.zeros((tall, channels), jnp.float32)
        for n in range(2 * parts):
            g = ups[n, at_w, :]
            squares = squares + g * g
        mean = jnp.sum(squares, axis=1, keepdims=True) / (2 * half)
        v = ups[mine, at_w, :] * lax.rsqrt(mean + 1e-06) * gain
        v = jnp.where(valid, v / (1.0 + jnp.exp(-v)), 0.0)
        above = jnp.where(h_row == 0, 0.0, pltpu.roll(v, 1, 0))
        below = jnp.where(h_row == height - 1, 0.0, pltpu.roll(v, tall - 1, 0))
        for b, line_v in enumerate((above, v, below)):
            wide[w + 1, :, b * channels : (b + 1) * channels] = line_v.astype(jnp.bfloat16)
        return carry

    lax.fori_loop(0, width, normalise, 0)
    loads[3].wait()

    span = frames * height

    def partial(d):
        total = jnp.zeros((columns * span, weight.shape[2]), jnp.float32)
        for a in range(3):
            for e in range(3):
                window = wide[pl.ds(d * columns + e, columns), a * height : a * height + span, :]
                taps = jnp.concatenate([weight[9 * a + 3 * b + e] for b in range(3)], axis=0)
                total = total + dot(window.reshape(columns * span, 3 * channels), taps)
        return total

    sums = []
    for k in [*range(sections // 2, sections), *range(1, sections // 2)]:
        d = lax.rem(sec + k, sections)
        send_buf[k] = partial(d).astype(jnp.bfloat16)
        c = pltpu.make_async_remote_copy(
            send_buf.at[k], recv_buf.at[k], sum_send.at[k], sum_recv.at[k],
            device_id={"section": d},
        )
        c.start()
        sums.append(c)
    total = partial(sec) + conv_bias[...]
    total = total.reshape(columns, span, half)
    own_w = []
    for w in range(columns):
        first = pl.multiple_of((sec * columns + w) * tall + 2 * height, height)
        own_w.append(
            jnp.concatenate([ups[n, pl.ds(first, span), :] for n in range(parts)], axis=1)
        )
    total = total + jnp.stack(own_w)
    for c in sums:
        c.wait()
    for k in range(1, sections):
        total = total + recv_buf[k].astype(jnp.float32).reshape(columns, span, half)
    for w in range(columns):
        for n in range(parts):
            final[n, pl.ds(w, span, stride=columns), :] = total[
                w, :, n * channels : (n + 1) * channels
            ]
    for n in range(parts):
        out[:, n * channels : (n + 1) * channels] = final[n].astype(out.dtype)


def fused_shards(sizes, *arrays):
    (
        hidden, modulation, time_embed, head_weight, head_bias, noisy, step_size, latent_mean,
        latent_std, in_weight, in_bias, norm_gain, conv_weight, conv_bias,
    ) = arrays
    sections, clips_sp, frames, height, columns, lat, channels = sizes
    rows_i, cols_j, half = height // 2, columns * sections // 2, in_weight.shape[2]
    width, near, tokens, lanes = columns * sections, frames + 2, hidden.shape[0], 4 * lat
    line_size = 8 * lat
    f32, bf16 = jnp.float32, jnp.bfloat16
    vmem, dma = pltpu.VMEM, pltpu.SemaphoreType.DMA
    in_vmem = pl.BlockSpec(memory_space=pltpu.VMEM)
    rows = columns * frames * height
    out = pl.pallas_call(
        functools.partial(block_kernel, sizes),
        out_shape=jax.ShapeDtypeStruct((rows, half), bf16),
        in_specs=[in_vmem] * 4
        + [pl.BlockSpec(memory_space=pltpu.SMEM)]
        + [in_vmem] * 5
        + [pl.BlockSpec(memory_space=pl.ANY)] * 4,
        out_specs=in_vmem,
        scratch_shapes=[
            vmem(hidden.shape, bf16),
            vmem(head_weight.shape[::-1], bf16),
            vmem(in_weight.shape, bf16),
            vmem((tokens, lanes), f32),
            vmem((tokens, 128), f32),
            vmem((8, lanes), f32),
            vmem((tokens, lanes), f32),
            vmem((tokens, 128), f32),
            vmem((8, lanes), f32),
            vmem(in_weight.shape, bf16),
            vmem((1, half), f32),
            vmem((2, sections, tokens // 2, 2 * lanes), bf16),
            vmem((sections, tokens // sections, lanes), bf16),
            vmem((frames, tokens // sections, lanes), bf16),
            vmem((cols_j + 2, 2 * frames, rows_i, line_size), f32),
            vmem(((cols_j + 2) * near * rows_i, 3 * line_size), bf16),
            vmem((2, 6 * line_size, 4 * half), bf16),
            vmem((2 * half // channels, width * near * height, channels), f32),
            vmem((width + 2, near * height, 3 * channels), bf16),
            vmem(conv_weight.shape, bf16),
            vmem((sections, rows, half), bf16),
            vmem((sections, rows, half), bf16),
            vmem((half // channels, rows, channels), f32),
            dma((4,)),
            dma((5,)),
            dma((5,)),
            dma((sections,)),
            dma((sections,)),
            dma((2, sections)),
            dma((2, sections)),
            dma((sections,)),
            dma((sections,)),
        ],
        compiler_params=pltpu.CompilerParams(collective_id=0, has_side_effects=True),
    )(
        modulation, time_embed[None], head_bias[None], noisy.reshape(-1, lat), step_size,
        latent_std[None], latent_mean[None], in_bias[None], norm_gain.reshape(-1, channels),
        conv_bias[None], hidden, head_weight.T, in_weight, conv_weight,
    )
    return out.reshape(frames, height, columns, half)


def dispatch(*arrays):
    hidden, noisy, in_weight, conv_weight = arrays[0], arrays[5], arrays[9], arrays[12]
    frames, height, columns, lat = noisy.shape
    sections, cores, clips_sp = (lax.axis_size(axis) for axis in ("section", "tp", "sp"))
    channels, half = conv_weight.shape[1:]
    whole_frame = hidden.shape[0] == height // 2 * (columns * sections // 2)
    if (
        whole_frame
        and cores == 2
        and clips_sp > 1
        and frames == sections
        and channels % 128 == 0
        and half % channels == 0
        and lat == 16
        and height == 16
    ):
        sizes = (sections, clips_sp, frames, height, columns, lat, channels)
        return fused_shards(sizes, *arrays)
    return shards(*arrays)


def solution(mesh):
    placed = (
        P(("groups", "sp", "section"), "tp"),
        P(None, "tp"),
        P(("groups", "tp")),
        P("tp", None),
        P(),
        P(("groups", "sp"), None, "section", None),
        P("groups"),
        P(),
        P(),
        P(None, None, "tp"),
        P("tp"),
        P(),
        P(None, "section", "tp"),
        P("tp"),
    )
    return jax.shard_map(
        dispatch,
        mesh=mesh,
        in_specs=placed,
        out_specs=P(("groups", "sp"), None, "section", "tp"),
        check_vma=False,
    )
```

profile of v0, /device:TPU:0, one launch (start us, length us, event | category | flops | bytes accessed | tf_op | source)
XLA Modules:
  0.0 32.2 jit_solution(7438514607187188730)
XLA Ops:
  0.7 29.9 %shard_map.136 = bf16[256,256]{1,0:T(8,128)(2,1)} custom-call(f32[2,3072]{1,0:T(2,128)} %modulation.1, f32[1,3072]{1,0:T(1,128)} %bitcast.11, f32[1,64]{1,0:T(1,128)} %bitcast.15, bf16[256,16]{1,0:T(8,128)(2,1)} %bitcast.10, f32[1]{0:T(128)S(6)} %copy.15.step_size, f32[1,16]{1,0:T(1,128)} %bitcast.16, f32[1,16]{1,0:T(1,128)} %bitcast.17, f32[1,256]{1,0:T(1,128)} %bitcast.13, ...), custom_call_target="tpu_custom_call" | custom-call | tf_op jit(solution)/shard_map/pallas_call | solution.py:500
  30.6 1.6 %reshape.11 = bf16[4,16,4,256]{3,2,1,0:T(4,128)(2,1)} reshape(bf16[256,256]{1,0:T(8,128)(2,1)} %shard_map.136) | data formatting | bytes 262144 | tf_op jit(solution)/shard_map/reshape | solution.py:548
where the time goes:
time: 32.4 us; the launch traced here: 32.2 us
  Pallas kernels  29.9 us (92%)
  local copies, waits for them, and re-layouts  1.6 us (5%)
  between operations  0.66 us (2%)
    pallas_call x1, Pallas kernels, fused_shards(): pl.pallas_call(functools.partial(block_kernel, sizes), out_shape=jax.Shap...  29.9 us
    reshape x1, local copies, waits for them, and re-layouts, fused_shards(): return out.reshape(frames, height, columns, half)  1.6 us

commit v1 on v0

v1 whole, which is shorter than its diff:
```python
import functools

import jax
import jax.numpy as jnp
from jax import lax
from jax.experimental import pallas as pl
from jax.experimental.pallas import tpu as pltpu
from jax.sharding import PartitionSpec as P

D = 6144


def padded_2(value, sides, width):
    for axis, dim in sides:
        count, length = (lax.axis_size(axis), value.shape[dim])
        up = [(i, (i + 1) % count) for i in range(count - 1)]
        down = [(j, i) for i, j in up]
        last = lax.slice_in_dim(value, length - width, length, axis=dim)
        leading = lax.slice_in_dim(value, 0, width, axis=dim)
        before = lax.ppermute(last, axis, up)
        after = lax.ppermute(leading, axis, down)
        value = jnp.concatenate([before, value, after], axis=dim)
    return value


def passed_along(value, axis, by):
    count = lax.axis_size(axis)
    pairs = [(i, i + by) for i in range(count) if 0 <= i + by < count]
    return lax.ppermute(value, axis, pairs)


def conv_taps(padded, weight, frames, height, columns):
    channels = padded.shape[3]
    result = jnp.zeros((frames * height * columns, weight.shape[2]), jnp.float32)
    for offset_time in range(3):
        for offset_row in range(3):
            slab = padded[offset_time : offset_time + frames, offset_row : offset_row + height]
            window = jnp.concatenate(
                [slab[:, :, 0:columns], slab[:, :, 1 : columns + 1], slab[:, :, 2 : columns + 2]],
                axis=3,
            )
            first = 9 * offset_time + 3 * offset_row
            taps = weight[first : first + 3].reshape(3 * channels, weight.shape[2])
            result = result + jnp.dot(
                window.reshape(-1, 3 * channels), taps, preferred_element_type=jnp.float32
            )
    return result


def activate(source, gain_vector):
    values = source.astype(jnp.float32)
    squares = jnp.mean(values * values, axis=-1, keepdims=True)
    return jax.nn.silu(values * lax.rsqrt(squares + 1e-06) * gain_vector).astype(jnp.bfloat16)


def pad_rows(source):
    return jnp.pad(source, ((0, 0), (1, 1), (0, 0), (0, 0)))


def shards(
    hidden,
    modulation,
    time_embed,
    head_weight,
    head_bias,
    noisy,
    step_size,
    latent_mean,
    latent_std,
    in_weight,
    in_bias,
    norm_gain,
    conv_weight,
    conv_bias,
):
    frames, height, columns, lat_channels = noisy.shape
    sections = lax.axis_size("section")
    half_channels = in_weight.shape[2]
    values = hidden.astype(jnp.float32)
    row_sums, square_sums = lax.psum(
        (jnp.sum(values, axis=1), jnp.sum(values * values, axis=1)), "tp"
    )
    average = row_sums / D
    variance = square_sums / D - average * average
    shift_term = modulation[0] + time_embed
    scale_term = modulation[1] + time_embed
    modulated = (
        (values - average[:, None]) * lax.rsqrt(variance[:, None] + 1e-06) * (1.0 + scale_term)
        + shift_term
    ).astype(jnp.bfloat16)
    partial_sum = jnp.dot(modulated, head_weight, preferred_element_type=jnp.float32)
    velocity = (lax.psum(partial_sum, "tp") + head_bias).astype(jnp.bfloat16)
    band_rows = velocity.shape[0] * 2 // (columns * sections)
    outgoing = velocity.reshape(band_rows, sections, -1)
    arrived = lax.all_to_all(outgoing, "section", split_axis=1, concat_axis=0, tiled=True)
    latent_field = arrived.reshape(frames, height // 2, columns // 2, 2, 2, lat_channels)
    latent_field = jnp.transpose(latent_field, (0, 1, 3, 2, 4, 5)).reshape(
        frames, height, columns, lat_channels
    )
    latent = (
        (noisy.astype(jnp.float32) - step_size[0] * latent_field.astype(jnp.float32)) * latent_std
        + latent_mean
    ).astype(jnp.bfloat16)
    latent_wide = padded_2(latent, (("section", 2),), 2)
    earlier = passed_along(latent_wide, "sp", 1)
    stacked = pad_rows(jnp.concatenate([earlier, latent_wide], axis=0))
    extended = (conv_taps(stacked, in_weight, frames + 2, height, columns + 2) + in_bias).astype(
        jnp.bfloat16
    )
    extended = extended.reshape(frames + 2, height, columns + 2, half_channels)
    upblock_half = extended[2:, :, 1 : columns + 1]
    extended_full = lax.all_gather(extended, "tp", axis=3, tiled=True)
    normed = activate(extended_full, norm_gain)
    frame_index = lax.axis_index("sp") * frames - 2 + jnp.arange(frames + 2, dtype=jnp.int32)
    column_index = (
        lax.axis_index("section") * columns - 1 + jnp.arange(columns + 2, dtype=jnp.int32)
    )
    inside_cols = (column_index >= 0) & (column_index < columns * sections)
    inside = (frame_index >= 0)[:, None, None, None] & inside_cols[None, None, :, None]
    conv_input = pad_rows(jnp.where(inside, normed, jnp.zeros_like(normed)))
    full_weight = lax.all_gather(conv_weight, "section", axis=1, tiled=True)
    mixed = conv_taps(conv_input, full_weight, frames, height, columns)
    decoded = (
        upblock_half.astype(jnp.float32).reshape(-1, half_channels) + mixed + conv_bias
    ).astype(jnp.bfloat16)
    return decoded.reshape(frames, height, columns, half_channels)


def iota(shape, dim):
    return lax.broadcasted_iota(jnp.int32, shape, dim)


def dot(left, right):
    return jnp.dot(left, right, preferred_element_type=jnp.float32)


def dot_rows(left, right):
    return lax.dot_general(
        left, right, (((1,), (1,)), ((), ())), preferred_element_type=jnp.float32
    )


def pieces(value):
    high = value.astype(jnp.bfloat16)
    rest = value - high.astype(jnp.float32)
    middle = rest.astype(jnp.bfloat16)
    low = (rest - middle.astype(jnp.float32)).astype(jnp.bfloat16)
    return high.astype(jnp.float32), middle.astype(jnp.float32), low.astype(jnp.float32)


def block_kernel(
    sizes,
    modulation_far,
    time_far,
    head_bias_far,
    noisy_far,
    step_size,
    std_far,
    mean_far,
    in_bias_far,
    gain_far,
    conv_bias_far,
    hidden_far,
    head_far,
    in_far,
    conv_far,
    out,
    modulation,
    time_embed,
    head_bias,
    noisy,
    latent_std,
    latent_mean,
    in_bias,
    norm_gain,
    conv_bias,
    hidden,
    head_weight,
    in_weight,
    weight,
    swap,
    noise_pick,
    noise_mask,
    places,
    part,
    peer_part,
    peer_weight,
    peer_bias,
    fields,
    noises,
    noise_lines,
    expanded,
    stacked,
    taps_in,
    ups,
    squares,
    wide,
    send_buf,
    recv_buf,
    held,
    acc,
    final,
    load_sems,
    pair_send,
    pair_recv,
    noise_send,
    noise_recv,
    field_send,
    field_recv,
    sum_send,
    sum_recv,
):
    sections, clips_sp, frames, height, columns, lat, channels = sizes
    rows_i, cols_j = height // 2, columns * sections // 2
    width = columns * sections
    tokens = rows_i * cols_j
    near = frames + 2
    half = in_weight.shape[2]
    lanes = 4 * lat
    folded = tokens // 2
    line_size = 4 * 2 * lat
    sec, core, spi = lax.axis_index("section"), lax.axis_index("tp"), lax.axis_index("sp")
    nxt = lax.rem(spi + 1, clips_sp)
    prv = lax.rem(spi + clips_sp - 1, clips_sp)
    has_next, has_prev = spi + 1 < clips_sp, spi > 0
    peer = {"tp": 1 - core}

    barrier = pltpu.get_barrier_semaphore()
    pl.semaphore_signal(barrier, inc=1, device_id=peer)
    for k in range(1, sections):
        pl.semaphore_signal(barrier, inc=1, device_id={"section": lax.rem(sec + k, sections)})

    @pl.when(has_prev)
    def _():
        for k in range(sections):
            pl.semaphore_signal(
                barrier, inc=1, device_id={"section": lax.rem(sec + k, sections), "sp": prv}
            )

    pairs = (
        (head_far, head_weight),
        (modulation_far, modulation),
        (time_far, time_embed),
        (hidden_far, hidden),
        (noisy_far, noisy),
        (in_far, in_weight),
        (in_bias_far, in_bias),
        (head_bias_far, head_bias),
        (std_far, latent_std),
        (mean_far, latent_mean),
        (gain_far, norm_gain),
        (conv_bias_far, conv_bias),
        (conv_far, weight),
    )
    loads = [
        pltpu.make_async_copy(source, target, load_sems.at[n])
        for n, (source, target) in enumerate(pairs)
    ]
    for c in loads:
        c.start()

    def pair_copy(n, source, target):
        return pltpu.make_async_remote_copy(
            source, target, pair_send.at[n], pair_recv.at[n], device_id=peer
        )

    def spread(target, send, recv):
        made, ahead = [], []
        source = target.at[0, 0]
        for k in range(1, sections):
            made.append(
                pltpu.make_async_remote_copy(
                    source, target.at[0, k], send.at[0, k], recv.at[0, k],
                    device_id={"section": lax.rem(sec + k, sections)},
                )
            )
        for k in range(sections):
            ahead.append(
                pltpu.make_async_remote_copy(
                    source, target.at[1, k], send.at[1, k], recv.at[1, k],
                    device_id={"section": lax.rem(sec + k, sections), "sp": nxt},
                )
            )
        return made, ahead

    def spread_start(copies):
        for c in copies[0]:
            c.start()

        @pl.when(has_next)
        def _():
            for c in copies[1]:
                c.start()

    def spread_wait(copies):
        for c in copies[0]:
            c.wait_recv()

        @pl.when(has_prev)
        def _():
            for c in copies[1]:
                c.wait_recv()

    def spread_drain(copies):
        for c in copies[0]:
            c.wait_send()

        @pl.when(has_next)
        def _():
            for c in copies[1]:
                c.wait_send()

    to, at = iota((tokens, tokens), 0), iota((tokens, tokens), 1)
    swap[...] = (lax.rem(to, rows_i) * cols_j + lax.div(to, rows_i) == at).astype(jnp.bfloat16)
    cells = frames * height * columns
    group = frames // 2
    r_line, r_col = lax.div(iota((cells, 2 * lanes), 0), columns), lax.rem(
        iota((cells, 2 * lanes), 0), columns
    )
    r_slot = lax.div(lax.div(r_line, height), group) * 4 + lax.rem(r_line, 2) * 2 + lax.rem(r_col, 2)
    noise_mask[...] = (lax.div(iota((cells, 2 * lanes), 1), lat) == r_slot).astype(jnp.float32)
    packed = cells // 8
    r_at, r_to = iota((packed, cells), 1), iota((packed, cells), 0)
    r_line, r_col = lax.div(r_at, columns), lax.rem(r_at, columns)
    r_home = (
        lax.rem(lax.div(r_line, height), group) * (columns // 2) + lax.div(r_col, 2)
    ) * rows_i + lax.div(lax.rem(r_line, height), 2)
    noise_pick[...] = (r_to == r_home).astype(jnp.bfloat16)
    shape = (2 * lanes, 2 * line_size)
    src, dst = iota(shape, 0), iota(shape, 1)
    same = lax.div(src, lanes) == lax.div(dst, line_size)
    src, dst = lax.rem(src, lanes), lax.rem(dst, line_size)
    places[0] = (same & (src == dst + 2 * lat) & (dst < 2 * lat)).astype(jnp.bfloat16)
    places[1] = (same & (src + 2 * lat == dst)).astype(jnp.bfloat16)
    places[2] = (same & (src + 6 * lat == dst) & (dst >= 6 * lat)).astype(jnp.bfloat16)
    expanded[...] = jnp.zeros_like(expanded)
    taps_in[...] = jnp.zeros_like(taps_in)
    wide[0] = jnp.zeros_like(wide[0])
    wide[width + 1] = jnp.zeros_like(wide[0])
    is_end = (sec == 0) | (sec == sections - 1)

    @pl.when(is_end)
    def _():
        recv_buf[3] = jnp.zeros_like(recv_buf[3])

    @pl.when(jnp.logical_not(has_prev))
    def _():
        fields[1] = jnp.zeros_like(fields[1])
        noises[1] = jnp.zeros_like(noises[1])

    features = hidden.shape[1]
    for c in loads[:3]:
        c.wait()
    scale = 1.0 + (modulation[1:2, :] + time_embed[...])
    shift = modulation[0:1, :] + time_embed[...]
    row = iota((16, features), 0)
    lines = jnp.zeros((16, features), jnp.float32)
    for n, piece in enumerate(pieces(scale) + pieces(shift)):
        lines = jnp.where(row == n, piece, lines)
    loads[3].wait()
    values = hidden[...].astype(jnp.float32)
    own_sum = jnp.sum(values, axis=1, keepdims=True)
    own_square = jnp.sum(values * values, axis=1, keepdims=True)
    center = own_sum / features
    centred = ((values - center) * scale).astype(jnp.bfloat16)
    stack = jnp.concatenate([centred, lines.astype(jnp.bfloat16)], axis=0)
    made = dot_rows(stack, head_weight[...])
    part[:tokens, :lanes] = made[:tokens]
    stat_shape = (tokens, 128 - lanes)
    part[:tokens, lanes:] = jnp.where(
        iota(stat_shape, 1) < stat_shape[1] // 2, own_sum, own_square
    )
    made = made[tokens:]
    line = iota(made.shape, 0)
    own_scale = jnp.sum(jnp.where(line < 3, made, 0.0), axis=0, keepdims=True)
    own_shift = jnp.sum(jnp.where(line < 3, 0.0, made), axis=0, keepdims=True)
    part[tokens:, :lanes] = jnp.where(iota((8, lanes), 0) == 0, own_scale, own_shift)
    part[tokens:, lanes:] = jnp.zeros((8, 128 - lanes), jnp.float32)
    pair = pair_copy(0, part, peer_part)
    early = [pair_copy(1, in_weight, peer_weight), pair_copy(2, in_bias, peer_bias)]
    pl.semaphore_wait(barrier, sections + jnp.where(has_next, sections, 0))
    pair.start()

    for c in loads[4:12]:
        c.wait()
    src, dst = iota((lat, 2 * lanes), 0), iota((lat, 2 * lanes), 1)
    tiled = dot(noisy[...], (src == lax.rem(dst, lat)).astype(jnp.bfloat16))
    tiled = (tiled * noise_mask[...]).astype(jnp.bfloat16)
    noises[0, 0] = dot(noise_pick[...], tiled).astype(jnp.bfloat16)
    noise_copies = spread(noises, noise_send, noise_recv)
    spread_start(noise_copies)
    for c in early:
        c.start()
    std = jnp.concatenate([latent_std[...]] * 8, axis=1)
    mean_latent = jnp.concatenate([latent_mean[...]] * 8, axis=1)
    pair.wait()
    far_sum = peer_part[:tokens, lanes : lanes + 1]
    far_square = peer_part[:tokens, lanes + (128 - lanes) // 2 : lanes + (128 - lanes) // 2 + 1]
    average = (own_sum + far_sum) / D
    variance = (own_square + far_square) / D - average * average
    body = (
        part[:tokens, :lanes]
        + peer_part[:tokens, :lanes]
        - (average - center) * own_scale
        - (average - far_sum / features) * peer_part[tokens : tokens + 1, :lanes]
    )
    velocity = (
        lax.rsqrt(variance + 1e-06) * body
        + (own_shift + peer_part[tokens + 1 : tokens + 2, :lanes])
        + head_bias[...]
    ).astype(jnp.bfloat16)
    field = dot(swap[...], velocity)
    fields[0, 0] = jnp.concatenate([field[:folded], field[folded:]], axis=1).astype(jnp.bfloat16)
    field_copies = spread(fields, field_send, field_recv)
    spread_start(field_copies)

    for c in early:
        c.wait()
    for q in range(2):
        for e in range(3):
            col = q + e
            step_j, odd = (col + 1) // 2 - q, (col + 1) % 2
            for a in range(3):
                for b in range(3):
                    tap = 9 * a + 3 * b + e
                    for p in range(2):
                        first = step_j * 3 * line_size + a * line_size + (p + b) * 2 * lat + odd * lat
                        left = p * 2 * half
                        taps_in[q, first : first + lat, left : left + half] = in_weight[tap]
                        taps_in[q, first : first + lat, left + half : left + 2 * half] = peer_weight[tap]
    spread_wait(noise_copies)
    lane = iota((folded, 2 * lanes), 1)
    side = folded // 2
    for slot in (1, 0):
        got = [
            noises[slot, lax.rem(sec + sections - g, sections)].astype(jnp.float32)
            for g in range(sections)
        ]
        for f in range(frames):
            r = f % group
            low, high = (
                jnp.concatenate(
                    [got[g][r * side : (r + 1) * side] for g in (2 * t, 2 * t + 1)], axis=0
                )
                for t in range(2)
            )
            if f < group:
                high = pltpu.roll(high, lanes, 1)
            else:
                low = pltpu.roll(low, lanes, 1)
            at_f = ((1 - slot) * frames + f) * folded
            noise_lines[at_f : at_f + folded, :] = jnp.where(lane < lanes, low, high)
    spread_wait(field_copies)

    lines_f = jnp.concatenate(
        [
            fields[slot, lax.rem(sec + sections - f, sections)]
            for slot in (1, 0)
            for f in range(frames)
        ],
        axis=0,
    ).astype(jnp.float32)
    lines_f = ((noise_lines[...] - step_size[0] * lines_f) * std + mean_latent).astype(
        jnp.bfloat16
    ).astype(jnp.float32)
    count = 2 * frames * folded
    f_row = iota((count, 2 * lanes), 0)
    i_row = lax.rem(f_row, rows_i)
    lines_f = jnp.where((f_row >= frames * folded) | has_prev, lines_f, 0.0)
    before = jnp.where(i_row == 0, 0.0, pltpu.roll(lines_f, 1, 0))
    after = jnp.where(i_row == rows_i - 1, 0.0, pltpu.roll(lines_f, count - 1, 0))
    line_values = (
        dot(before.astype(jnp.bfloat16), places[0])
        + dot(lines_f.astype(jnp.bfloat16), places[1])
        + dot(after.astype(jnp.bfloat16), places[2])
    )
    half_j = cols_j // 2
    for f in range(2 * frames):
        for side in range(2):
            expanded[1 + side * half_j : 1 + (side + 1) * half_j, f] = line_values[
                f * folded : (f + 1) * folded, side * line_size : (side + 1) * line_size
            ].reshape(half_j, rows_i, line_size)
    block = near * rows_i
    for j in range(cols_j + 2):
        for a in range(3):
            stacked[j * block : (j + 1) * block, a * line_size : (a + 1) * line_size] = (
                expanded[j, a : a + near].reshape(block, line_size).astype(jnp.bfloat16)
            )
    parts = half // channels
    tall = near * height
    for q in range(2):
        lhs = jnp.concatenate(
            [
                stacked[q * block : (q + cols_j) * block, :],
                stacked[(q + 1) * block : (q + 1 + cols_j) * block, :],
            ],
            axis=1,
        )
        for p in range(2):
            total = jnp.zeros((cols_j * block, channels), jnp.float32)
            for h in range(2):
                left = (p * 2 + h) * half
                bias = in_bias[...] if h == 0 else peer_bias[...]
                up = dot(lhs, taps_in[q, :, left : left + half]) + bias
                up = up.astype(jnp.bfloat16).astype(jnp.float32)
                for n in range(parts):
                    chunk = up[:, n * channels : (n + 1) * channels]
                    total = total + chunk * chunk
                for j in range(cols_j):
                    for n in range(parts):
                        ups[
                            h * parts + n, pl.ds((2 * j + q) * tall + p, block, stride=2), :
                        ] = up[j * block : (j + 1) * block, n * channels : (n + 1) * channels]
            for j in range(cols_j):
                squares[pl.ds((2 * j + q) * tall + p, block, stride=2), :] = total[
                    j * block : (j + 1) * block
                ]

    mine = lax.rem(sec + parts * core, 2 * parts)
    gain = norm_gain[pl.ds(sec, 1), :]
    h_row = lax.rem(iota((tall, channels), 0), height)
    valid = has_prev | (iota((tall, channels), 0) >= 2 * height)

    def normalise(w):
        at_w = pl.ds(pl.multiple_of(w * tall, tall), tall)
        mean = jnp.sum(squares[at_w, :], axis=1, keepdims=True) / (2 * half)
        v = ups[mine, at_w, :] * lax.rsqrt(mean + 1e-06) * gain
        v = jnp.where(valid, v / (1.0 + jnp.exp(-v)), 0.0)
        above = jnp.where(h_row == 0, 0.0, pltpu.roll(v, 1, 0))
        below = jnp.where(h_row == height - 1, 0.0, pltpu.roll(v, tall - 1, 0))
        for b, line_v in enumerate((above, v, below)):
            wide[w + 1, :, b * channels : (b + 1) * channels] = line_v.astype(jnp.bfloat16)

    span = frames * height
    pair_columns = columns // 2
    rows = pair_columns * span

    def partial(d, m):
        windows, taps = [], []
        for a in range(3):
            for e in range(3):
                window = wide[
                    pl.ds(d * columns + e + m * pair_columns, pair_columns),
                    a * height : a * height + span,
                    :,
                ]
                windows.append(window.reshape(rows, 3 * channels))
                taps += [weight[9 * a + 3 * b + e] for b in range(3)]
        return dot(jnp.concatenate(windows, axis=1), jnp.concatenate(taps, axis=0))

    up_side = sec < sections // 2
    away = jnp.where(up_side, sec, sections - 1 - sec)

    def mirrored(value):
        return jnp.where(up_side, value, sections - 1 - value)

    inner = jnp.logical_not(is_end)
    dests = [
        mirrored(jnp.where(is_end, sections - 1, sections // 2)),
        mirrored(jnp.where(is_end, sections - 2, 0)),
        mirrored(jnp.where(is_end, 1, sections - 1)),
    ]
    hop = mirrored(jnp.where(is_end, 1, sections // 2))
    first_slot = jnp.where(is_end, 0, 3)

    def sum_copy(n, m):
        slot = first_slot if n == 0 else n
        return pltpu.make_async_remote_copy(
            send_buf.at[n, m], recv_buf.at[slot, m], sum_send.at[n, m], sum_recv.at[slot, m],
            device_id={"section": hop if n == 0 else dests[n]},
        )

    def arrival(slot, m):
        return pltpu.make_async_remote_copy(
            send_buf.at[0, m], recv_buf.at[slot, m], sum_send.at[0, m], sum_recv.at[slot, m],
            device_id={"section": hop},
        )

    for t in range(columns + 2):
        normalise(lax.rem(dests[0] * columns + width - 1 + t, width))
    loads[12].wait()
    for m in range(2):
        send_buf[0, m] = partial(dests[0], m).astype(jnp.bfloat16)
        sum_copy(0, m).start()
    for t in range(width - columns - 2):
        normalise(lax.rem(dests[0] * columns + columns + 1 + t, width))
    for m in range(2):
        send_buf[1, m] = partial(dests[1], m).astype(jnp.bfloat16)
        sum_copy(1, m).start()
    for m in range(2):
        value = partial(dests[2], m)

        @pl.when(is_end)
        def _():
            send_buf[2, m] = value.astype(jnp.bfloat16)
            sum_copy(2, m).start()

        @pl.when(inner)
        def _():
            held[m] = value

    for m in range(2):
        value = partial(sec, m) + conv_bias[...]
        residual = []
        for w in range(pair_columns):
            first = pl.multiple_of(
                (sec * columns + m * pair_columns + w) * tall + 2 * height, height
            )
            residual.append(
                jnp.concatenate([ups[n, pl.ds(first, span), :] for n in range(parts)], axis=1)
            )
        acc[m] = value + jnp.concatenate(residual, axis=0)

    @pl.when(inner)
    def _():
        for m in range(2):
            arrival(0, m).wait_recv()
            send_buf[2, m] = (held[m] + recv_buf[0, m].astype(jnp.float32)).astype(jnp.bfloat16)
            sum_copy(2, m).start()
        for m in range(2):
            arrival(3, m).wait_recv()

    for m in range(2):
        arrival(1, m).wait_recv()
        acc[m] = (
            acc[m] + recv_buf[1, m].astype(jnp.float32) + recv_buf[3, m].astype(jnp.float32)
        )
    for m in range(2):
        arrival(2, m).wait_recv()
        total = acc[m] + recv_buf[2, m].astype(jnp.float32)
        for w in range(pair_columns):
            for n in range(parts):
                final[n, pl.ds(m * pair_columns + w, span, stride=columns), :] = total[
                    w * span : (w + 1) * span, n * channels : (n + 1) * channels
                ]
    for n in range(parts):
        out[:, n * channels : (n + 1) * channels] = final[n].astype(out.dtype)
    for n in range(3):
        for m in range(2):
            sum_copy(n, m).wait_send()
    spread_drain(noise_copies)
    spread_drain(field_copies)


def fused_shards(sizes, *arrays):
    (
        hidden, modulation, time_embed, head_weight, head_bias, noisy, step_size, latent_mean,
        latent_std, in_weight, in_bias, norm_gain, conv_weight, conv_bias,
    ) = arrays
    sections, clips_sp, frames, height, columns, lat, channels = sizes
    rows_i, cols_j, half = height // 2, columns * sections // 2, in_weight.shape[2]
    width, near, tokens, lanes = columns * sections, frames + 2, hidden.shape[0], 4 * lat
    line_size = 8 * lat
    f32, bf16 = jnp.float32, jnp.bfloat16
    vmem, dma = pltpu.VMEM, pltpu.SemaphoreType.DMA
    rows = columns * frames * height
    operands = (
        modulation, time_embed[None], head_bias[None], noisy.reshape(-1, lat),
        latent_std[None], latent_mean[None], in_bias[None], norm_gain.reshape(-1, channels),
        conv_bias[None], hidden, head_weight.T, in_weight, conv_weight,
    )
    operands = [pltpu.with_memory_space_constraint(value, pltpu.HBM) for value in operands]
    far = pl.BlockSpec(memory_space=pltpu.HBM)
    out = pl.pallas_call(
        functools.partial(block_kernel, sizes),
        out_shape=pltpu.VMEM((rows, half), bf16),
        in_specs=[far] * 4
        + [pl.BlockSpec(memory_space=pltpu.SMEM)]
        + [far] * (len(operands) - 4),
        out_specs=pl.BlockSpec(memory_space=pltpu.VMEM),
        scratch_shapes=[vmem(value.shape, value.dtype) for value in operands]
        + [
            vmem((tokens, tokens), bf16),
            vmem((rows // 8, rows), bf16),
            vmem((rows, 2 * lanes), f32),
            vmem((3, 2 * lanes, 2 * line_size), bf16),
            vmem((tokens + 8, 128), f32),
            vmem((tokens + 8, 128), f32),
            vmem(in_weight.shape, bf16),
            vmem((1, half), f32),
            vmem((2, sections, tokens // 2, 2 * lanes), bf16),
            vmem((2, sections, rows // 8, 2 * lanes), bf16),
            vmem((2 * frames * tokens // 2, 2 * lanes), f32),
            vmem((cols_j + 2, 2 * frames, rows_i, line_size), f32),
            vmem(((cols_j + 2) * near * rows_i, 3 * line_size), bf16),
            vmem((2, 6 * line_size, 4 * half), bf16),
            vmem((2 * half // channels, width * near * height, channels), f32),
            vmem((width * near * height, channels), f32),
            vmem((width + 2, near * height, 3 * channels), bf16),
            vmem((3, 2, rows // 2, half), bf16),
            vmem((4, 2, rows // 2, half), bf16),
            vmem((2, rows // 2, half), f32),
            vmem((2, rows // 2, half), f32),
            vmem((half // channels, rows, channels), f32),
            dma((len(operands),)),
            dma((3,)),
            dma((3,)),
            dma((2, sections)),
            dma((2, sections)),
            dma((2, sections)),
            dma((2, sections)),
            dma((3, 2)),
            dma((4, 2)),
        ],
        compiler_params=pltpu.CompilerParams(
            collective_id=0, has_side_effects=True, vmem_limit_bytes=40 * 2**20
        ),
    )(*operands[:4], step_size, *operands[4:])
    return out.reshape(frames, height, columns, half)


def dispatch(*arrays):
    hidden, noisy, in_weight, conv_weight = arrays[0], arrays[5], arrays[9], arrays[12]
    frames, height, columns, lat = noisy.shape
    sections, cores, clips_sp = (lax.axis_size(axis) for axis in ("section", "tp", "sp"))
    channels, half = conv_weight.shape[1:]
    whole_frame = hidden.shape[0] == height // 2 * (columns * sections // 2)
    if (
        whole_frame
        and cores == 2
        and clips_sp > 1
        and frames == sections
        and sections == 4
        and columns % 2 == 0
        and channels % 128 == 0
        and half % channels == 0
        and lat == 16
        and height == 16
    ):
        sizes = (sections, clips_sp, frames, height, columns, lat, channels)
        return fused_shards(sizes, *arrays)
    return shards(*arrays)


def solution(mesh):
    placed = (
        P(("groups", "sp", "section"), "tp"),
        P(None, "tp"),
        P(("groups", "tp")),
        P("tp", None),
        P(),
        P(("groups", "sp"), None, "section", None),
        P("groups"),
        P(),
        P(),
        P(None, None, "tp"),
        P("tp"),
        P(),
        P(None, "section", "tp"),
        P("tp"),
    )
    return jax.shard_map(
        dispatch,
        mesh=mesh,
        in_specs=placed,
        out_specs=P(("groups", "sp"), None, "section", "tp"),
        check_vma=False,
    )
```

time: 32.4 us -> 26.1 us (0.81)
  Pallas kernels: 29.9 us -> 24.6 us
  local copies, waits for them, and re-layouts: 1.6 us -> 0.69 us
    pallas_call x1, Pallas kernels: 29.9 us -> 24.6 us  [fused_shards(): pl.pallas_call(functools.partial(block_kernel, sizes), out_shape=pltpu.VM...]
    reshape x1, local copies, waits for them, and re-layouts: 1.6 us -> 0.69 us  [fused_shards(): return out.reshape(frames, height, columns, half)]
where the time goes in v1:
time: 26.1 us; the launch traced here: 26 us
  Pallas kernels  24.6 us (94%)
  local copies, waits for them, and re-layouts  0.69 us (3%)
  between operations  0.66 us (3%)
    pallas_call x1, Pallas kernels, fused_shards(): pl.pallas_call(functools.partial(block_kernel, sizes), out_shape=pltpu.VM...  24.6 us
    reshape x1, local copies, waits for them, and re-layouts, fused_shards(): return out.reshape(frames, height, columns, half)  0.69 us

profile of v1, /device:TPU:0, one launch (start us, length us, event | category | flops | bytes accessed | tf_op | source)
XLA Modules:
  0.0 26.0 jit_solution(9622744999084558270)
XLA Ops:
  0.7 24.6 %shard_map.136 = bf16[256,256]{1,0:T(8,128)(2,1)S(1)} custom-call(f32[2,3072]{1,0:T(2,128)} %modulation_far.1, f32[1,3072]{1,0:T(1,128)} %bitcast.11, f32[1,64]{1,0:T(1,128)} %bitcast.15, bf16[256,16]{1,0:T(8,128)(2,1)} %bitcast.10, f32[1]{0:T(128)S(6)} %copy.15.step_size, f32[1,16]{1,0:T(1,128)} %bitcast.16, f32[1,16]{1,0:T(1,128)} %bitcast.17, ...), custom_call_target="tpu_custom_call" | custom-call | tf_op jit(solution)/shard_map/pallas_call | solution.py:664
  25.3 0.7 %reshape.11 = bf16[4,16,4,256]{3,2,1,0:T(4,128)(2,1)} reshape(bf16[256,256]{1,0:T(8,128)(2,1)S(1)} %shard_map.136) | data formatting | bytes 262144 | tf_op jit(solution)/shard_map/reshape | solution.py:709

commit v2 on v1

--- a/solution.py
+++ b/solution.py
@@ -187,7 +187,6 @@
     peer_weight,
     peer_bias,
     fields,
-    noises,
     noise_lines,
     expanded,
     stacked,
@@ -203,8 +202,6 @@
     load_sems,
     pair_send,
     pair_recv,
-    noise_send,
-    noise_recv,
     field_send,
     field_recv,
     sum_send,
@@ -225,38 +222,52 @@
     has_next, has_prev = spi + 1 < clips_sp, spi > 0
     peer = {"tp": 1 - core}
 
+    lead = core == 1
     barrier = pltpu.get_barrier_semaphore()
     pl.semaphore_signal(barrier, inc=1, device_id=peer)
     for k in range(1, sections):
-        pl.semaphore_signal(barrier, inc=1, device_id={"section": lax.rem(sec + k, sections)})
+        pl.semaphore_signal(
+            barrier, inc=1, device_id={"section": lax.rem(sec + k, sections), "tp": 1}
+        )
 
     @pl.when(has_prev)
     def _():
         for k in range(sections):
             pl.semaphore_signal(
-                barrier, inc=1, device_id={"section": lax.rem(sec + k, sections), "sp": prv}
+                barrier,
+                inc=1,
+                device_id={"section": lax.rem(sec + k, sections), "sp": prv, "tp": 1},
             )
 
-    pairs = (
-        (head_far, head_weight),
-        (modulation_far, modulation),
-        (time_far, time_embed),
-        (hidden_far, hidden),
-        (noisy_far, noisy),
-        (in_far, in_weight),
-        (in_bias_far, in_bias),
-        (head_bias_far, head_bias),
-        (std_far, latent_std),
-        (mean_far, latent_mean),
-        (gain_far, norm_gain),
-        (conv_bias_far, conv_bias),
-        (conv_far, weight),
+
+    def quarters(ref):
+        size = ref.shape[0] // 4
+        return [pl.ds(n * size, size) for n in range(4)]
+
+    groups = (
+        (
+            *((head_far.at[part_of], head_weight.at[part_of]) for part_of in quarters(head_far)),
+            (modulation_far, modulation),
+            (time_far, time_embed),
+            *((hidden_far.at[part_of], hidden.at[part_of]) for part_of in quarters(hidden_far)),
+        ),
+        (
+            (noisy_far, noisy),
+            (in_bias_far, in_bias),
+            (head_bias_far, head_bias),
+            (std_far, latent_std),
+            (mean_far, latent_mean),
+            (gain_far, norm_gain),
+            (conv_bias_far, conv_bias),
+            (in_far, in_weight),
+        ),
+        ((conv_far, weight),),
     )
     loads = [
-        pltpu.make_async_copy(source, target, load_sems.at[n])
-        for n, (source, target) in enumerate(pairs)
+        [pltpu.make_async_copy(source, target, load_sems.at[n]) for source, target in members]
+        for n, members in enumerate(groups)
     ]
-    for c in loads:
+    for c in loads[0] + loads[1]:
         c.start()
 
     def pair_copy(n, source, target):
@@ -264,51 +275,42 @@
             source, target, pair_send.at[n], pair_recv.at[n], device_id=peer
         )
 
-    def spread(target, send, recv):
-        made, ahead = [], []
-        source = target.at[0, 0]
-        for k in range(1, sections):
-            made.append(
-                pltpu.make_async_remote_copy(
-                    source, target.at[0, k], send.at[0, k], recv.at[0, k],
-                    device_id={"section": lax.rem(sec + k, sections)},
-                )
-            )
-        for k in range(sections):
-            ahead.append(
-                pltpu.make_async_remote_copy(
-                    source, target.at[1, k], send.at[1, k], recv.at[1, k],
-                    device_id={"section": lax.rem(sec + k, sections), "sp": nxt},
-                )
-            )
-        return made, ahead
-
-    def spread_start(copies):
-        for c in copies[0]:
-            c.start()
-
-        @pl.when(has_next)
-        def _():
-            for c in copies[1]:
-                c.start()
-
-    def spread_wait(copies):
-        for c in copies[0]:
-            c.wait_recv()
-
-        @pl.when(has_prev)
-        def _():
-            for c in copies[1]:
-                c.wait_recv()
-
-    def spread_drain(copies):
-        for c in copies[0]:
-            c.wait_send()
-
-        @pl.when(has_next)
-        def _():
-            for c in copies[1]:
-                c.wait_send()
+    def wait_rows(count, sem):
+        view = ups.at[0, pl.ds(0, count), :]
+        pltpu.make_async_copy(view, view, sem).wait()
+
+    up_side = sec < sections // 2
+    is_end = (sec == 0) | (sec == sections - 1)
+    inner = jnp.logical_not(is_end)
+
+    def mirrored(value):
+        return jnp.where(up_side, value, sections - 1 - value)
+
+    others = [mirrored(jnp.where(is_end, sections - 1 - n, (3, 2, 0)[n])) for n in range(3)]
+
+    def spread_copy(z, ahead, c):
+        slot = lax.rem(z - sec + sections, sections)
+        return pltpu.make_async_remote_copy(
+            fields.at[0, 0], fields.at[ahead, slot], field_send.at[0], field_recv.at[0],
+            device_id={"section": z, "sp": nxt if ahead else spi, "tp": c},
+        )
+
+    def spread():
+        for z in [*others, sec]:
+            if z is not sec:
+                for c in (1, 0):
+                    spread_copy(z, 0, c).start()
+
+            @pl.when(has_next)
+            def _():
+                for c in (1, 0):
+                    spread_copy(z, 1, c).start()
+
+        pltpu.make_async_remote_copy(
+            fields.at[0, 0], fields.at[0, 0], field_send.at[0], field_recv.at[0], device_id=peer
+        ).start()
+
+    field_rows = 2 * folded * 2 * lanes * 2 // 512
 
     to, at = iota((tokens, tokens), 0), iota((tokens, tokens), 1)
     swap[...] = (lax.rem(to, rows_i) * cols_j + lax.div(to, rows_i) == at).astype(jnp.bfloat16)
@@ -337,27 +339,21 @@
     taps_in[...] = jnp.zeros_like(taps_in)
     wide[0] = jnp.zeros_like(wide[0])
     wide[width + 1] = jnp.zeros_like(wide[0])
-    is_end = (sec == 0) | (sec == sections - 1)
-
-    @pl.when(is_end)
-    def _():
-        recv_buf[3] = jnp.zeros_like(recv_buf[3])
 
     @pl.when(jnp.logical_not(has_prev))
     def _():
         fields[1] = jnp.zeros_like(fields[1])
-        noises[1] = jnp.zeros_like(noises[1])
 
     features = hidden.shape[1]
-    for c in loads[:3]:
+    for c in loads[0]:
         c.wait()
+    loads[2][0].start()
     scale = 1.0 + (modulation[1:2, :] + time_embed[...])
     shift = modulation[0:1, :] + time_embed[...]
     row = iota((16, features), 0)
     lines = jnp.zeros((16, features), jnp.float32)
     for n, piece in enumerate(pieces(scale) + pieces(shift)):
         lines = jnp.where(row == n, piece, lines)
-    loads[3].wait()
     values = hidden[...].astype(jnp.float32)
     own_sum = jnp.sum(values, axis=1, keepdims=True)
     own_square = jnp.sum(values * values, axis=1, keepdims=True)
@@ -378,44 +374,55 @@
     part[tokens:, lanes:] = jnp.zeros((8, 128 - lanes), jnp.float32)
     pair = pair_copy(0, part, peer_part)
     early = [pair_copy(1, in_weight, peer_weight), pair_copy(2, in_bias, peer_bias)]
-    pl.semaphore_wait(barrier, sections + jnp.where(has_next, sections, 0))
-    pair.start()
-
-    for c in loads[4:12]:
+    for c in loads[1]:
         c.wait()
-    src, dst = iota((lat, 2 * lanes), 0), iota((lat, 2 * lanes), 1)
-    tiled = dot(noisy[...], (src == lax.rem(dst, lat)).astype(jnp.bfloat16))
-    tiled = (tiled * noise_mask[...]).astype(jnp.bfloat16)
-    noises[0, 0] = dot(noise_pick[...], tiled).astype(jnp.bfloat16)
-    noise_copies = spread(noises, noise_send, noise_recv)
-    spread_start(noise_copies)
-    for c in early:
-        c.start()
     std = jnp.concatenate([latent_std[...]] * 8, axis=1)
     mean_latent = jnp.concatenate([latent_mean[...]] * 8, axis=1)
-    pair.wait()
-    far_sum = peer_part[:tokens, lanes : lanes + 1]
-    far_square = peer_part[:tokens, lanes + (128 - lanes) // 2 : lanes + (128 - lanes) // 2 + 1]
-    average = (own_sum + far_sum) / D
-    variance = (own_square + far_square) / D - average * average
-    body = (
-        part[:tokens, :lanes]
-        + peer_part[:tokens, :lanes]
-        - (average - center) * own_scale
-        - (average - far_sum / features) * peer_part[tokens : tokens + 1, :lanes]
-    )
-    velocity = (
-        lax.rsqrt(variance + 1e-06) * body
-        + (own_shift + peer_part[tokens + 1 : tokens + 2, :lanes])
-        + head_bias[...]
-    ).astype(jnp.bfloat16)
-    field = dot(swap[...], velocity)
-    fields[0, 0] = jnp.concatenate([field[:folded], field[folded:]], axis=1).astype(jnp.bfloat16)
-    field_copies = spread(fields, field_send, field_recv)
-    spread_start(field_copies)
+
+    @pl.when(core == 0)
+    def _():
+        pl.semaphore_wait(barrier, 1)
+        pair.start()
+        for c in early:
+            c.start()
+
+    @pl.when(lead)
+    def _():
+        src, dst = iota((lat, 2 * lanes), 0), iota((lat, 2 * lanes), 1)
+        tiled = dot(noisy[...], (src == lax.rem(dst, lat)).astype(jnp.bfloat16))
+        tiled = (tiled * noise_mask[...]).astype(jnp.bfloat16)
+        fields[0, 0, 1] = dot(noise_pick[...], tiled).astype(jnp.bfloat16)
+        pair.wait_recv()
+        far_sum = peer_part[:tokens, lanes : lanes + 1]
+        far_square = peer_part[
+            :tokens, lanes + (128 - lanes) // 2 : lanes + (128 - lanes) // 2 + 1
+        ]
+        average = (own_sum + far_sum) / D
+        variance = (own_square + far_square) / D - average * average
+        body = (
+            part[:tokens, :lanes]
+            + peer_part[:tokens, :lanes]
+            - (average - center) * own_scale
+            - (average - far_sum / features) * peer_part[tokens : tokens + 1, :lanes]
+        )
+        velocity = (
+            lax.rsqrt(variance + 1e-06) * body
+            + (own_shift + peer_part[tokens + 1 : tokens + 2, :lanes])
+            + head_bias[...]
+        ).astype(jnp.bfloat16)
+        field = dot(swap[...], velocity)
+        fields[0, 0, 0] = jnp.concatenate([field[:folded], field[folded:]], axis=1).astype(
+            jnp.bfloat16
+        )
+        pl.semaphore_wait(
+            barrier, 2 * sections - 1 + jnp.where(has_next, 2 * sections, 0)
+        )
+        spread()
+        for c in early:
+            c.start()
 
     for c in early:
-        c.wait()
+        c.wait_recv()
     for q in range(2):
         for e in range(3):
             col = q + e
@@ -428,12 +435,20 @@
                         left = p * 2 * half
                         taps_in[q, first : first + lat, left : left + half] = in_weight[tap]
                         taps_in[q, first : first + lat, left + half : left + 2 * half] = peer_weight[tap]
-    spread_wait(noise_copies)
+
+    for on_lead in (True, False):
+        for first in (True, False):
+
+            @pl.when((lead == on_lead) & (has_prev != first))
+            def _():
+                count = sections - 1 + (0 if first else sections) + (0 if on_lead else 1)
+                wait_rows(count * field_rows, field_recv.at[0])
+
     lane = iota((folded, 2 * lanes), 1)
     side = folded // 2
     for slot in (1, 0):
         got = [
-            noises[slot, lax.rem(sec + sections - g, sections)].astype(jnp.float32)
+            fields[slot, lax.rem(sec + sections - g, sections), 1].astype(jnp.float32)
             for g in range(sections)
         ]
         for f in range(frames):
@@ -450,11 +465,10 @@
                 low = pltpu.roll(low, lanes, 1)
             at_f = ((1 - slot) * frames + f) * folded
             noise_lines[at_f : at_f + folded, :] = jnp.where(lane < lanes, low, high)
-    spread_wait(field_copies)
 
     lines_f = jnp.concatenate(
         [
-            fields[slot, lax.rem(sec + sections - f, sections)]
+            fields[slot, lax.rem(sec + sections - f, sections), 0]
             for slot in (1, 0)
             for f in range(frames)
         ],
@@ -486,35 +500,56 @@
             stacked[j * block : (j + 1) * block, a * line_size : (a + 1) * line_size] = (
                 expanded[j, a : a + near].reshape(block, line_size).astype(jnp.bfloat16)
             )
+    dests = [
+        jnp.where(is_end, mirrored(sections - 1), 0),
+        mirrored(sections - 2),
+        jnp.where(is_end, mirrored(1), sections - 1),
+    ]
     parts = half // channels
     tall = near * height
-    for q in range(2):
-        lhs = jnp.concatenate(
-            [
-                stacked[q * block : (q + cols_j) * block, :],
-                stacked[(q + 1) * block : (q + 1 + cols_j) * block, :],
-            ],
-            axis=1,
-        )
-        for p in range(2):
-            total = jnp.zeros((cols_j * block, channels), jnp.float32)
-            for h in range(2):
-                left = (p * 2 + h) * half
-                bias = in_bias[...] if h == 0 else peer_bias[...]
-                up = dot(lhs, taps_in[q, :, left : left + half]) + bias
-                up = up.astype(jnp.bfloat16).astype(jnp.float32)
-                for n in range(parts):
-                    chunk = up[:, n * channels : (n + 1) * channels]
-                    total = total + chunk * chunk
-                for j in range(cols_j):
+
+    def upblock(homes):
+        for q in range(2):
+            lhs = jnp.concatenate(
+                [
+                    jnp.concatenate(
+                        [
+                            stacked[pl.ds(pl.multiple_of((j + q + n) * block, block), block), :]
+                            for n in range(2)
+                        ],
+                        axis=1,
+                    )
+                    for j in homes
+                ],
+                axis=0,
+            )
+            for p in range(2):
+                total = jnp.zeros((len(homes) * block, channels), jnp.float32)
+                for h in range(2):
+                    left = (p * 2 + h) * half
+                    bias = in_bias[...] if h == 0 else peer_bias[...]
+                    up = dot(lhs, taps_in[q, :, left : left + half]) + bias
+                    up = up.astype(jnp.bfloat16).astype(jnp.float32)
                     for n in range(parts):
-                        ups[
-                            h * parts + n, pl.ds((2 * j + q) * tall + p, block, stride=2), :
-                        ] = up[j * block : (j + 1) * block, n * channels : (n + 1) * channels]
-            for j in range(cols_j):
-                squares[pl.ds((2 * j + q) * tall + p, block, stride=2), :] = total[
-                    j * block : (j + 1) * block
-                ]
+                        chunk = up[:, n * channels : (n + 1) * channels]
+                        total = total + chunk * chunk
+                    for m, j in enumerate(homes):
+                        at_j = pl.ds(pl.multiple_of(2 * j * tall, tall) + q * tall + p, block, stride=2)
+                        for n in range(parts):
+                            ups[h * parts + n, at_j, :] = up[
+                                m * block : (m + 1) * block, n * channels : (n + 1) * channels
+                            ]
+                for m, j in enumerate(homes):
+                    at_j = pl.ds(pl.multiple_of(2 * j * tall, tall) + q * tall + p, block, stride=2)
+                    squares[at_j, :] = total[m * block : (m + 1) * block]
+
+    def homes_from(first):
+        return [
+            lax.rem(dests[0] * columns // 2 + cols_j + first + n, cols_j)
+            for n in range(cols_j // 2)
+        ]
+
+    upblock(homes_from(-1))
 
     mine = lax.rem(sec + parts * core, 2 * parts)
     gain = norm_gain[pl.ds(sec, 1), :]
@@ -534,6 +569,8 @@
     span = frames * height
     pair_columns = columns // 2
     rows = pair_columns * span
+
+    unit = jnp.where(core >= 0, 1.0, 0.0)
 
     def partial(d, m):
         windows, taps = [], []
@@ -546,58 +583,61 @@
                 ]
                 windows.append(window.reshape(rows, 3 * channels))
                 taps += [weight[9 * a + 3 * b + e] for b in range(3)]
-        return dot(jnp.concatenate(windows, axis=1), jnp.concatenate(taps, axis=0))
-
-    up_side = sec < sections // 2
-    away = jnp.where(up_side, sec, sections - 1 - sec)
-
-    def mirrored(value):
-        return jnp.where(up_side, value, sections - 1 - value)
-
-    inner = jnp.logical_not(is_end)
-    dests = [
-        mirrored(jnp.where(is_end, sections - 1, sections // 2)),
-        mirrored(jnp.where(is_end, sections - 2, 0)),
-        mirrored(jnp.where(is_end, 1, sections - 1)),
-    ]
-    hop = mirrored(jnp.where(is_end, 1, sections // 2))
-    first_slot = jnp.where(is_end, 0, 3)
-
-    def sum_copy(n, m):
-        slot = first_slot if n == 0 else n
+        low, high = (
+            dot(
+                jnp.concatenate(windows[first:last], axis=1),
+                jnp.concatenate(taps[3 * first : 3 * last], axis=0),
+            )
+            for first, last in ((0, 5), (5, 9))
+        )
+        return low + high * unit
+
+    neighbour = mirrored(1)
+    far_slot = jnp.where(up_side, 2, 0)
+    targets = [dests[0], jnp.where(is_end, neighbour, dests[1]), dests[2]]
+    slots = [jnp.where(is_end, 1, far_slot), jnp.where(is_end, 3, 1), jnp.where(is_end, 2, 2 - far_slot)]
+
+    def sum_copy(n, w):
         return pltpu.make_async_remote_copy(
-            send_buf.at[n, m], recv_buf.at[slot, m], sum_send.at[n, m], sum_recv.at[slot, m],
-            device_id={"section": hop if n == 0 else dests[n]},
+            send_buf.at[n, w], recv_buf.at[slots[n], w], sum_send.at[0],
+            sum_recv.at[slots[n], w], device_id={"section": targets[n]},
         )
 
-    def arrival(slot, m):
-        return pltpu.make_async_remote_copy(
-            send_buf.at[0, m], recv_buf.at[slot, m], sum_send.at[0, m], sum_recv.at[slot, m],
-            device_id={"section": hop},
-        )
+    def arrived(slot, w):
+        pltpu.make_async_copy(
+            recv_buf.at[slot, w], recv_buf.at[slot, w], sum_recv.at[slot, w]
+        ).wait()
+        return recv_buf[slot, w].astype(jnp.float32)
+
+    def by_column(value):
+        return [value[w * span : (w + 1) * span] for w in range(pair_columns)]
 
     for t in range(columns + 2):
         normalise(lax.rem(dests[0] * columns + width - 1 + t, width))
-    loads[12].wait()
+    loads[2][0].wait()
     for m in range(2):
-        send_buf[0, m] = partial(dests[0], m).astype(jnp.bfloat16)
-        sum_copy(0, m).start()
+        for w, value in enumerate(by_column(partial(dests[0], m))):
+            send_buf[0, m * pair_columns + w] = value.astype(jnp.bfloat16)
+        for w in range(pair_columns):
+            sum_copy(0, m * pair_columns + w).start()
+    upblock(homes_from(cols_j // 2 - 1))
     for t in range(width - columns - 2):
         normalise(lax.rem(dests[0] * columns + columns + 1 + t, width))
     for m in range(2):
-        send_buf[1, m] = partial(dests[1], m).astype(jnp.bfloat16)
-        sum_copy(1, m).start()
+        for w, value in enumerate(by_column(partial(dests[1], m))):
+            held[m * pair_columns + w] = value
+
+    @pl.when(is_end)
+    def _():
+        send_buf[1] = held[...].astype(jnp.bfloat16)
+        for w in range(columns):
+            sum_copy(1, w).start()
+
     for m in range(2):
-        value = partial(dests[2], m)
-
-        @pl.when(is_end)
-        def _():
-            send_buf[2, m] = value.astype(jnp.bfloat16)
-            sum_copy(2, m).start()
-
-        @pl.when(inner)
-        def _():
-            held[m] = value
+        for w, value in enumerate(by_column(partial(dests[2], m))):
+            send_buf[2, m * pair_columns + w] = value.astype(jnp.bfloat16)
+    for w in range(columns):
+        sum_copy(2, w).start()
 
     for m in range(2):
         value = partial(sec, m) + conv_bias[...]
@@ -609,37 +649,51 @@
             residual.append(
                 jnp.concatenate([ups[n, pl.ds(first, span), :] for n in range(parts)], axis=1)
             )
-        acc[m] = value + jnp.concatenate(residual, axis=0)
+        for w, own in enumerate(by_column(value)):
+            acc[m * pair_columns + w] = own + residual[w]
 
     @pl.when(inner)
     def _():
-        for m in range(2):
-            arrival(0, m).wait_recv()
-            send_buf[2, m] = (held[m] + recv_buf[0, m].astype(jnp.float32)).astype(jnp.bfloat16)
-            sum_copy(2, m).start()
-        for m in range(2):
-            arrival(3, m).wait_recv()
-
-    for m in range(2):
-        arrival(1, m).wait_recv()
-        acc[m] = (
-            acc[m] + recv_buf[1, m].astype(jnp.float32) + recv_buf[3, m].astype(jnp.float32)
-        )
-    for m in range(2):
-        arrival(2, m).wait_recv()
-        total = acc[m] + recv_buf[2, m].astype(jnp.float32)
-        for w in range(pair_columns):
-            for n in range(parts):
-                final[n, pl.ds(m * pair_columns + w, span, stride=columns), :] = total[
-                    w * span : (w + 1) * span, n * channels : (n + 1) * channels
+        for w in range(columns):
+            send_buf[1, w] = (held[w] + arrived(3, w)).astype(jnp.bfloat16)
+            sum_copy(1, w).start()
+
+
+    def finish(order):
+        for n in order[:-1]:
+            for w in range(columns):
+                acc[w] = acc[w] + arrived(n, w)
+        for w in range(columns):
+            total = acc[w] + arrived(order[-1], w)
+            for c in range(parts):
+                final[c, pl.ds(w, span, stride=columns), :] = total[
+                    :, c * channels : (c + 1) * channels
                 ]
+
+    @pl.when(is_end)
+    def _():
+        finish((2, 0, 1))
+
+    @pl.when(inner)
+    def _():
+        finish((2, 1))
+
     for n in range(parts):
         out[:, n * channels : (n + 1) * channels] = final[n].astype(out.dtype)
-    for n in range(3):
-        for m in range(2):
-            sum_copy(n, m).wait_send()
-    spread_drain(noise_copies)
-    spread_drain(field_copies)
+    wait_rows(3 * columns * span * half * 2 // 512, sum_send.at[0])
+    for c in early:
+        c.wait_send()
+
+    @pl.when(core == 0)
+    def _():
+        pair.wait_send()
+
+    for first in (True, False):
+
+        @pl.when(lead & (has_next != first))
+        def _():
+            count = 2 * (sections - 1) + (0 if first else 2 * sections) + 1
+            wait_rows(count * field_rows, field_send.at[0])
 
 
 def fused_shards(sizes, *arrays):
@@ -678,8 +732,7 @@
             vmem((tokens + 8, 128), f32),
             vmem(in_weight.shape, bf16),
             vmem((1, half), f32),
-            vmem((2, sections, tokens // 2, 2 * lanes), bf16),
-            vmem((2, sections, rows // 8, 2 * lanes), bf16),
+            vmem((2, sections, 2, tokens // 2, 2 * lanes), bf16),
             vmem((2 * frames * tokens // 2, 2 * lanes), f32),
             vmem((cols_j + 2, 2 * frames, rows_i, line_size), f32),
             vmem(((cols_j + 2) * near * rows_i, 3 * line_size), bf16),
@@ -687,20 +740,18 @@
             vmem((2 * half // channels, width * near * height, channels), f32),
             vmem((width * near * height, channels), f32),
             vmem((width + 2, near * height, 3 * channels), bf16),
-            vmem((3, 2, rows // 2, half), bf16),
-            vmem((4, 2, rows // 2, half), bf16),
-            vmem((2, rows // 2, half), f32),
-            vmem((2, rows // 2, half), f32),
+            vmem((3, columns, rows // columns, half), bf16),
+            vmem((4, columns, rows // columns, half), bf16),
+            vmem((columns, rows // columns, half), f32),
+            vmem((columns, rows // columns, half), f32),
             vmem((half // channels, rows, channels), f32),
-            dma((len(operands),)),
             dma((3,)),
             dma((3,)),
-            dma((2, sections)),
-            dma((2, sections)),
-            dma((2, sections)),
-            dma((2, sections)),
-            dma((3, 2)),
-            dma((4, 2)),
+            dma((3,)),
+            dma((1,)),
+            dma((1,)),
+            dma((1,)),
+            dma((4, columns)),
         ],
         compiler_params=pltpu.CompilerParams(
             collective_id=0, has_side_effects=True, vmem_limit_bytes=40 * 2**20

time: 26.1 us -> 24 us (0.920)
  Pallas kernels: 24.6 us -> 22.5 us
    pallas_call x1, Pallas kernels: 24.6 us -> 22.5 us  [fused_shards(): pl.pallas_call(functools.partial(block_kernel, sizes), out_shape=pltpu.VM...]
where the time goes in v2:
time: 24 us; the launch traced here: 23.8 us
  Pallas kernels  22.5 us (94%)
  local copies, waits for them, and re-layouts  0.69 us (3%)
  between operations  0.66 us (3%)
    pallas_call x1, Pallas kernels, fused_shards(): pl.pallas_call(functools.partial(block_kernel, sizes), out_shape=pltpu.VM...  22.5 us
    reshape x1, local copies, waits for them, and re-layouts, fused_shards(): return out.reshape(frames, height, columns, half)  0.69 us

profile of v2, /device:TPU:0, one launch (start us, length us, event | category | flops | bytes accessed | tf_op | source)
XLA Modules:
  0.0 23.8 jit_solution(2489970898918757612)
XLA Ops:
  0.7 22.5 %shard_map.136 = bf16[256,256]{1,0:T(8,128)(2,1)S(1)} custom-call(f32[2,3072]{1,0:T(2,128)} %modulation_far.1, f32[1,3072]{1,0:T(1,128)} %bitcast.11, f32[1,64]{1,0:T(1,128)} %bitcast.15, bf16[256,16]{1,0:T(8,128)(2,1)} %bitcast.10, f32[1]{0:T(128)S(6)} %copy.15.step_size, f32[1,16]{1,0:T(1,128)} %bitcast.16, f32[1,16]{1,0:T(1,128)} %bitcast.17, ...), custom_call_target="tpu_custom_call" | custom-call | tf_op jit(solution)/shard_map/pallas_call | solution.py:718
  23.1 0.7 %reshape.11 = bf16[4,16,4,256]{3,2,1,0:T(4,128)(2,1)} reshape(bf16[256,256]{1,0:T(8,128)(2,1)S(1)} %shard_map.136) | data formatting | bytes 262144 | tf_op jit(solution)/shard_map/reshape | solution.py:760

commit v3 on v2

--- a/solution.py
+++ b/solution.py
@@ -240,17 +240,9 @@
             )
 
 
-    def quarters(ref):
-        size = ref.shape[0] // 4
-        return [pl.ds(n * size, size) for n in range(4)]
-
     groups = (
-        (
-            *((head_far.at[part_of], head_weight.at[part_of]) for part_of in quarters(head_far)),
-            (modulation_far, modulation),
-            (time_far, time_embed),
-            *((hidden_far.at[part_of], hidden.at[part_of]) for part_of in quarters(hidden_far)),
-        ),
+        ((hidden_far, hidden),),
+        ((modulation_far, modulation), (time_far, time_embed), (head_far, head_weight)),
         (
             (noisy_far, noisy),
             (in_bias_far, in_bias),
@@ -267,7 +259,7 @@
         [pltpu.make_async_copy(source, target, load_sems.at[n]) for source, target in members]
         for n, members in enumerate(groups)
     ]
-    for c in loads[0] + loads[1]:
+    for c in loads[1] + loads[0] + loads[2]:
         c.start()
 
     def pair_copy(n, source, target):
@@ -345,21 +337,23 @@
         fields[1] = jnp.zeros_like(fields[1])
 
     features = hidden.shape[1]
-    for c in loads[0]:
+    for c in loads[1]:
         c.wait()
-    loads[2][0].start()
     scale = 1.0 + (modulation[1:2, :] + time_embed[...])
     shift = modulation[0:1, :] + time_embed[...]
-    row = iota((16, features), 0)
-    lines = jnp.zeros((16, features), jnp.float32)
+    row = iota((8, features), 0)
+    lines = jnp.zeros((8, features), jnp.float32)
     for n, piece in enumerate(pieces(scale) + pieces(shift)):
         lines = jnp.where(row == n, piece, lines)
+    lines = jnp.concatenate([lines, jnp.zeros_like(lines)], axis=0).astype(jnp.bfloat16)
+    loads[0][0].wait()
+    loads[3][0].start()
     values = hidden[...].astype(jnp.float32)
     own_sum = jnp.sum(values, axis=1, keepdims=True)
     own_square = jnp.sum(values * values, axis=1, keepdims=True)
     center = own_sum / features
     centred = ((values - center) * scale).astype(jnp.bfloat16)
-    stack = jnp.concatenate([centred, lines.astype(jnp.bfloat16)], axis=0)
+    stack = jnp.concatenate([centred, lines], axis=0)
     made = dot_rows(stack, head_weight[...])
     part[:tokens, :lanes] = made[:tokens]
     stat_shape = (tokens, 128 - lanes)
@@ -374,7 +368,7 @@
     part[tokens:, lanes:] = jnp.zeros((8, 128 - lanes), jnp.float32)
     pair = pair_copy(0, part, peer_part)
     early = [pair_copy(1, in_weight, peer_weight), pair_copy(2, in_bias, peer_bias)]
-    for c in loads[1]:
+    for c in loads[2]:
         c.wait()
     std = jnp.concatenate([latent_std[...]] * 8, axis=1)
     mean_latent = jnp.concatenate([latent_mean[...]] * 8, axis=1)
@@ -502,8 +496,8 @@
             )
     dests = [
         jnp.where(is_end, mirrored(sections - 1), 0),
-        mirrored(sections - 2),
-        jnp.where(is_end, mirrored(1), sections - 1),
+        jnp.where(is_end, mirrored(sections - 2), sections - 1),
+        mirrored(jnp.where(is_end, 1, sections - 2)),
     ]
     parts = half // channels
     tall = near * height
@@ -593,9 +587,14 @@
         return low + high * unit
 
     neighbour = mirrored(1)
-    far_slot = jnp.where(up_side, 2, 0)
-    targets = [dests[0], jnp.where(is_end, neighbour, dests[1]), dests[2]]
-    slots = [jnp.where(is_end, 1, far_slot), jnp.where(is_end, 3, 1), jnp.where(is_end, 2, 2 - far_slot)]
+    targets = [jnp.where(is_end, neighbour, d) for d in dests]
+    far_n = jnp.where(up_side, 1, 0)
+    slots = [
+        jnp.where(is_end, 2, 1 - far_n),
+        jnp.where(is_end, 3, far_n),
+        jnp.where(is_end, 0, 1),
+    ]
+    direct = [is_end | up_side, is_end | jnp.logical_not(up_side), is_end]
 
     def sum_copy(n, w):
         return pltpu.make_async_remote_copy(
@@ -603,6 +602,19 @@
             sum_recv.at[slots[n], w], device_id={"section": targets[n]},
         )
 
+    def far_copy(w):
+        return pltpu.make_async_remote_copy(
+            send_buf.at[far_n, w], recv_buf.at[1, w], sum_send.at[0], sum_recv.at[1, w],
+            device_id={"section": mirrored(sections - 1)},
+        )
+
+    def relay_far(*pieces_w):
+        @pl.when(inner)
+        def _():
+            for w in pieces_w:
+                send_buf[far_n, w] = (held[far_n, w] + arrived(2, w)).astype(jnp.bfloat16)
+                far_copy(w).start()
+
     def arrived(slot, w):
         pltpu.make_async_copy(
             recv_buf.at[slot, w], recv_buf.at[slot, w], sum_recv.at[slot, w]
@@ -614,30 +626,33 @@
 
     for t in range(columns + 2):
         normalise(lax.rem(dests[0] * columns + width - 1 + t, width))
-    loads[2][0].wait()
+    loads[3][0].wait()
+    def hold(n, m):
+        for c, value in enumerate(by_column(partial(dests[n], m))):
+            w = m * pair_columns + c
+            send_buf[n, w] = value.astype(jnp.bfloat16)
+            held[n, w] = value
+
+    def send(n, pieces_w):
+        @pl.when(direct[n])
+        def _():
+            for w in pieces_w:
+                sum_copy(n, w).start()
+
     for m in range(2):
-        for w, value in enumerate(by_column(partial(dests[0], m))):
-            send_buf[0, m * pair_columns + w] = value.astype(jnp.bfloat16)
-        for w in range(pair_columns):
-            sum_copy(0, m * pair_columns + w).start()
+        hold(0, m)
+        send(0, range(m * pair_columns, (m + 1) * pair_columns))
     upblock(homes_from(cols_j // 2 - 1))
     for t in range(width - columns - 2):
         normalise(lax.rem(dests[0] * columns + columns + 1 + t, width))
     for m in range(2):
-        for w, value in enumerate(by_column(partial(dests[1], m))):
-            held[m * pair_columns + w] = value
-
-    @pl.when(is_end)
-    def _():
-        send_buf[1] = held[...].astype(jnp.bfloat16)
-        for w in range(columns):
-            sum_copy(1, w).start()
-
+        hold(1, m)
+    send(1, range(columns))
+    relay_far(0)
     for m in range(2):
-        for w, value in enumerate(by_column(partial(dests[2], m))):
-            send_buf[2, m * pair_columns + w] = value.astype(jnp.bfloat16)
-    for w in range(columns):
-        sum_copy(2, w).start()
+        hold(2, m)
+    send(2, range(columns))
+    relay_far(1, 2)
 
     for m in range(2):
         value = partial(sec, m) + conv_bias[...]
@@ -652,11 +667,13 @@
         for w, own in enumerate(by_column(value)):
             acc[m * pair_columns + w] = own + residual[w]
 
+    relay_far(*range(3, columns))
+
     @pl.when(inner)
     def _():
         for w in range(columns):
-            send_buf[1, w] = (held[w] + arrived(3, w)).astype(jnp.bfloat16)
-            sum_copy(1, w).start()
+            send_buf[2, w] = (held[2, w] + arrived(3, w)).astype(jnp.bfloat16)
+            sum_copy(2, w).start()
 
 
     def finish(order):
@@ -672,11 +689,11 @@
 
     @pl.when(is_end)
     def _():
-        finish((2, 0, 1))
+        finish((0, 1))
 
     @pl.when(inner)
     def _():
-        finish((2, 1))
+        finish((1, 0))
 
     for n in range(parts):
         out[:, n * channels : (n + 1) * channels] = final[n].astype(out.dtype)
@@ -742,10 +759,10 @@
             vmem((width + 2, near * height, 3 * channels), bf16),
             vmem((3, columns, rows // columns, half), bf16),
             vmem((4, columns, rows // columns, half), bf16),
-            vmem((columns, rows // columns, half), f32),
+            vmem((3, columns, rows // columns, half), f32),
             vmem((columns, rows // columns, half), f32),
             vmem((half // channels, rows, channels), f32),
-            dma((3,)),
+            dma((4,)),
             dma((3,)),
             dma((3,)),
             dma((1,)),

time: 24 us -> 22.9 us (0.954); the launches traced: 23.8 us -> 22.4 us
  Pallas kernels: 22.5 us -> 21.1 us
    pallas_call x1, Pallas kernels: 22.5 us -> 21.1 us  [fused_shards(): pl.pallas_call(functools.partial(block_kernel, sizes), out_shape=pltpu.VM...]
where the time goes in v3:
time: 22.9 us; the launch traced here: 22.4 us
  Pallas kernels  21.1 us (92%)
  local copies, waits for them, and re-layouts  0.69 us (3%)
  between operations  0.66 us (3%)
    pallas_call x1, Pallas kernels, fused_shards(): pl.pallas_call(functools.partial(block_kernel, sizes), out_shape=pltpu.VM...  21.1 us
    reshape x1, local copies, waits for them, and re-layouts, fused_shards(): return out.reshape(frames, height, columns, half)  0.69 us

profile of v3, /device:TPU:0, one launch (start us, length us, event | category | flops | bytes accessed | tf_op | source)
XLA Modules:
  0.0 22.4 jit_solution(10933376687240740490)
XLA Ops:
  0.7 21.1 %shard_map.136 = bf16[256,256]{1,0:T(8,128)(2,1)S(1)} custom-call(f32[2,3072]{1,0:T(2,128)} %modulation_far.1, f32[1,3072]{1,0:T(1,128)} %bitcast.11, f32[1,64]{1,0:T(1,128)} %bitcast.15, bf16[256,16]{1,0:T(8,128)(2,1)} %bitcast.10, f32[1]{0:T(128)S(6)} %copy.15.step_size, f32[1,16]{1,0:T(1,128)} %bitcast.16, f32[1,16]{1,0:T(1,128)} %bitcast.17, ...), custom_call_target="tpu_custom_call" | custom-call | tf_op jit(solution)/shard_map/pallas_call | solution.py:735
  21.7 0.7 %reshape.11 = bf16[4,16,4,256]{3,2,1,0:T(4,128)(2,1)} reshape(bf16[256,256]{1,0:T(8,128)(2,1)S(1)} %shard_map.136) | data formatting | bytes 262144 | tf_op jit(solution)/shard_map/reshape | solution.py:777

commit v4 on v3

--- a/solution.py
+++ b/solution.py
@@ -223,6 +223,7 @@
     peer = {"tp": 1 - core}
 
     lead = core == 1
+    unit = jnp.where(core >= 0, 1.0, 0.0)
     barrier = pltpu.get_barrier_semaphore()
     pl.semaphore_signal(barrier, inc=1, device_id=peer)
     for k in range(1, sections):
@@ -241,8 +242,8 @@
 
 
     groups = (
-        ((hidden_far, hidden),),
-        ((modulation_far, modulation), (time_far, time_embed), (head_far, head_weight)),
+        ((hidden_far, hidden), (head_far, head_weight)),
+        ((modulation_far, modulation), (time_far, time_embed)),
         (
             (noisy_far, noisy),
             (in_bias_far, in_bias),
@@ -251,9 +252,9 @@
             (mean_far, latent_mean),
             (gain_far, norm_gain),
             (conv_bias_far, conv_bias),
-            (in_far, in_weight),
         ),
         ((conv_far, weight),),
+        ((in_far, in_weight),),
     )
     loads = [
         [pltpu.make_async_copy(source, target, load_sems.at[n]) for source, target in members]
@@ -289,13 +290,12 @@
 
     def spread():
         for z in [*others, sec]:
-            if z is not sec:
-                for c in (1, 0):
+            for c in (0, 1):
+                if z is not sec:
                     spread_copy(z, 0, c).start()
 
-            @pl.when(has_next)
-            def _():
-                for c in (1, 0):
+                @pl.when(has_next)
+                def _():
                     spread_copy(z, 1, c).start()
 
         pltpu.make_async_remote_copy(
@@ -324,9 +324,9 @@
     src, dst = iota(shape, 0), iota(shape, 1)
     same = lax.div(src, lanes) == lax.div(dst, line_size)
     src, dst = lax.rem(src, lanes), lax.rem(dst, line_size)
-    places[0] = (same & (src == dst + 2 * lat) & (dst < 2 * lat)).astype(jnp.bfloat16)
-    places[1] = (same & (src + 2 * lat == dst)).astype(jnp.bfloat16)
-    places[2] = (same & (src + 6 * lat == dst) & (dst >= 6 * lat)).astype(jnp.bfloat16)
+    places[0 * shape[0] : (0 + 1) * shape[0]] = (same & (src == dst + 2 * lat) & (dst < 2 * lat)).astype(jnp.bfloat16)
+    places[1 * shape[0] : (1 + 1) * shape[0]] = (same & (src + 2 * lat == dst)).astype(jnp.bfloat16)
+    places[2 * shape[0] : (2 + 1) * shape[0]] = (same & (src + 6 * lat == dst) & (dst >= 6 * lat)).astype(jnp.bfloat16)
     expanded[...] = jnp.zeros_like(expanded)
     taps_in[...] = jnp.zeros_like(taps_in)
     wide[0] = jnp.zeros_like(wide[0])
@@ -346,7 +346,9 @@
     for n, piece in enumerate(pieces(scale) + pieces(shift)):
         lines = jnp.where(row == n, piece, lines)
     lines = jnp.concatenate([lines, jnp.zeros_like(lines)], axis=0).astype(jnp.bfloat16)
-    loads[0][0].wait()
+    for c in loads[0]:
+        c.wait()
+    loads[4][0].start()
     loads[3][0].start()
     values = hidden[...].astype(jnp.float32)
     own_sum = jnp.sum(values, axis=1, keepdims=True)
@@ -354,7 +356,9 @@
     center = own_sum / features
     centred = ((values - center) * scale).astype(jnp.bfloat16)
     stack = jnp.concatenate([centred, lines], axis=0)
-    made = dot_rows(stack, head_weight[...])
+    cut = features // 2
+    made = dot_rows(stack[:, :cut], head_weight[:, :cut])
+    made = made + dot_rows(stack[:, cut:], head_weight[:, cut:]) * unit
     part[:tokens, :lanes] = made[:tokens]
     stat_shape = (tokens, 128 - lanes)
     part[:tokens, lanes:] = jnp.where(
@@ -377,6 +381,7 @@
     def _():
         pl.semaphore_wait(barrier, 1)
         pair.start()
+        loads[4][0].wait()
         for c in early:
             c.start()
 
@@ -412,6 +417,7 @@
             barrier, 2 * sections - 1 + jnp.where(has_next, 2 * sections, 0)
         )
         spread()
+        loads[4][0].wait()
         for c in early:
             c.start()
 
@@ -477,10 +483,13 @@
     lines_f = jnp.where((f_row >= frames * folded) | has_prev, lines_f, 0.0)
     before = jnp.where(i_row == 0, 0.0, pltpu.roll(lines_f, 1, 0))
     after = jnp.where(i_row == rows_i - 1, 0.0, pltpu.roll(lines_f, count - 1, 0))
-    line_values = (
-        dot(before.astype(jnp.bfloat16), places[0])
-        + dot(lines_f.astype(jnp.bfloat16), places[1])
-        + dot(after.astype(jnp.bfloat16), places[2])
+    shifted = jnp.concatenate([before, lines_f, after], axis=1).astype(jnp.bfloat16)
+    line_values = jnp.concatenate(
+        [
+            dot(shifted[n * count // 2 : (n + 1) * count // 2], places[...])
+            for n in range(2)
+        ],
+        axis=0,
     )
     half_j = cols_j // 2
     for f in range(2 * frames):
@@ -537,13 +546,9 @@
                     at_j = pl.ds(pl.multiple_of(2 * j * tall, tall) + q * tall + p, block, stride=2)
                     squares[at_j, :] = total[m * block : (m + 1) * block]
 
-    def homes_from(first):
-        return [
-            lax.rem(dests[0] * columns // 2 + cols_j + first + n, cols_j)
-            for n in range(cols_j // 2)
-        ]
-
-    upblock(homes_from(-1))
+    edge_high = dests[0] > 0
+    first_home = jnp.where(edge_high, cols_j - 2, 0)
+    upblock([first_home, first_home + 1])
 
     mine = lax.rem(sec + parts * core, 2 * parts)
     gain = norm_gain[pl.ds(sec, 1), :]
@@ -562,20 +567,17 @@
 
     span = frames * height
     pair_columns = columns // 2
-    rows = pair_columns * span
-
-    unit = jnp.where(core >= 0, 1.0, 0.0)
-
-    def partial(d, m):
+
+    def partial(d, first_column, count):
         windows, taps = [], []
         for a in range(3):
             for e in range(3):
                 window = wide[
-                    pl.ds(d * columns + e + m * pair_columns, pair_columns),
+                    pl.ds(d * columns + e + first_column, count),
                     a * height : a * height + span,
                     :,
                 ]
-                windows.append(window.reshape(rows, 3 * channels))
+                windows.append(window.reshape(count * span, 3 * channels))
                 taps += [weight[9 * a + 3 * b + e] for b in range(3)]
         low, high = (
             dot(
@@ -584,7 +586,8 @@
             )
             for first, last in ((0, 5), (5, 9))
         )
-        return low + high * unit
+        value = low + high * unit
+        return [value[w * span : (w + 1) * span] for w in range(count)]
 
     neighbour = mirrored(1)
     targets = [jnp.where(is_end, neighbour, d) for d in dests]
@@ -608,10 +611,11 @@
             device_id={"section": mirrored(sections - 1)},
         )
 
-    def relay_far(*pieces_w):
-        @pl.when(inner)
+    def relay_far(side, *pieces_w):
+        @pl.when(inner & (up_side if side else jnp.logical_not(up_side)))
         def _():
-            for w in pieces_w:
+            for n in pieces_w:
+                w = jnp.where(up_side, (2, 3, 1, 0)[n], n)
                 send_buf[far_n, w] = (held[far_n, w] + arrived(2, w)).astype(jnp.bfloat16)
                 far_copy(w).start()
 
@@ -621,17 +625,21 @@
         ).wait()
         return recv_buf[slot, w].astype(jnp.float32)
 
-    def by_column(value):
-        return [value[w * span : (w + 1) * span] for w in range(pair_columns)]
-
-    for t in range(columns + 2):
-        normalise(lax.rem(dests[0] * columns + width - 1 + t, width))
+    for t in range(4):
+        normalise(2 * first_home + t)
+
+    later = [4, *range(width - 1, width - 2 - columns, -1), *range(5, width - 1 - columns)]
+
+    def normalise_next(numbers):
+        for n in numbers:
+            inward = jnp.where(edge_high, width - 5 - n, 4 + n)
+            normalise(jnp.where(is_end, inward, later[n]))
+
     loads[3][0].wait()
-    def hold(n, m):
-        for c, value in enumerate(by_column(partial(dests[n], m))):
-            w = m * pair_columns + c
-            send_buf[n, w] = value.astype(jnp.bfloat16)
-            held[n, w] = value
+    def hold(n, first_column, count):
+        for c, value in enumerate(partial(dests[n], first_column, count)):
+            send_buf[n, first_column + c] = value.astype(jnp.bfloat16)
+            held[n, first_column + c] = value
 
     def send(n, pieces_w):
         @pl.when(direct[n])
@@ -639,23 +647,33 @@
             for w in pieces_w:
                 sum_copy(n, w).start()
 
+    first_pair = jnp.where(edge_high, columns - 2, 0)
+    third, fourth = jnp.where(edge_high, 1, 2), jnp.where(edge_high, 0, 3)
+    hold(0, first_pair, 2)
+    send(0, (first_pair, first_pair + 1))
+    hold(0, third, 1)
+    send(0, (third,))
+    upblock([lax.rem(first_home + 2 + n, cols_j) for n in range(cols_j - 2)])
+    normalise_next((0,))
+    hold(0, fourth, 1)
+    send(0, (fourth,))
+    normalise_next(range(1, columns + 2))
+    relay_far(False, 0)
     for m in range(2):
-        hold(0, m)
-        send(0, range(m * pair_columns, (m + 1) * pair_columns))
-    upblock(homes_from(cols_j // 2 - 1))
-    for t in range(width - columns - 2):
-        normalise(lax.rem(dests[0] * columns + columns + 1 + t, width))
+        hold(1, m * pair_columns, pair_columns)
+        send(1, range(m * pair_columns, (m + 1) * pair_columns))
+    relay_far(False, 1)
+    normalise_next(range(columns + 2, width - 4))
+    relay_far(False, 2)
+    relay_far(True, 0)
     for m in range(2):
-        hold(1, m)
-    send(1, range(columns))
-    relay_far(0)
+        hold(2, m * pair_columns, pair_columns)
+    send(2, range(columns))
+    relay_far(False, 3)
+    relay_far(True, 1)
+
     for m in range(2):
-        hold(2, m)
-    send(2, range(columns))
-    relay_far(1, 2)
-
-    for m in range(2):
-        value = partial(sec, m) + conv_bias[...]
+        values = partial(sec, m * pair_columns, pair_columns)
         residual = []
         for w in range(pair_columns):
             first = pl.multiple_of(
@@ -664,10 +682,10 @@
             residual.append(
                 jnp.concatenate([ups[n, pl.ds(first, span), :] for n in range(parts)], axis=1)
             )
-        for w, own in enumerate(by_column(value)):
-            acc[m * pair_columns + w] = own + residual[w]
-
-    relay_far(*range(3, columns))
+        for w, own in enumerate(values):
+            acc[m * pair_columns + w] = own + conv_bias[...] + residual[w]
+
+    relay_far(True, 2, 3)
 
     @pl.when(inner)
     def _():
@@ -686,6 +704,7 @@
                 final[c, pl.ds(w, span, stride=columns), :] = total[
                     :, c * channels : (c + 1) * channels
                 ]
+
 
     @pl.when(is_end)
     def _():
@@ -744,7 +763,7 @@
             vmem((tokens, tokens), bf16),
             vmem((rows // 8, rows), bf16),
             vmem((rows, 2 * lanes), f32),
-            vmem((3, 2 * lanes, 2 * line_size), bf16),
+            vmem((6 * lanes, 2 * line_size), bf16),
             vmem((tokens + 8, 128), f32),
             vmem((tokens + 8, 128), f32),
             vmem(in_weight.shape, bf16),
@@ -762,7 +781,7 @@
             vmem((3, columns, rows // columns, half), f32),
             vmem((columns, rows // columns, half), f32),
             vmem((half // channels, rows, channels), f32),
-            dma((4,)),
+            dma((5,)),
             dma((3,)),
             dma((3,)),
             dma((1,)),
@@ -789,7 +808,7 @@
         and clips_sp > 1
         and frames == sections
         and sections == 4
-        and columns % 2 == 0
+        and columns == 4
         and channels % 128 == 0
         and half % channels == 0
         and lat == 16

time: 22.9 us -> 22.6 us (0.987)
  the two profiles are of different devices: /device:TPU:0 before, /device:TPU:19 now
where the time goes in v4:
time: 22.6 us; the launch traced here: 22.4 us
  Pallas kernels  21.1 us (93%)
  local copies, waits for them, and re-layouts  0.69 us (3%)
  between operations  0.66 us (3%)
    pallas_call x1, Pallas kernels, fused_shards(): pl.pallas_call(functools.partial(block_kernel, sizes), out_shape=pltpu.VM...  21.1 us
    reshape x1, local copies, waits for them, and re-layouts, fused_shards(): return out.reshape(frames, height, columns, half)  0.69 us

profile of v4, /device:TPU:19, one launch (start us, length us, event | category | flops | bytes accessed | tf_op | source)
XLA Modules:
  0.0 22.4 jit_solution(242412627620983730)
XLA Ops:
  0.7 21.1 %shard_map.136 = bf16[256,256]{1,0:T(8,128)(2,1)S(1)} custom-call(f32[2,3072]{1,0:T(2,128)} %modulation_far.1, f32[1,3072]{1,0:T(1,128)} %bitcast.11, f32[1,64]{1,0:T(1,128)} %bitcast.15, bf16[256,16]{1,0:T(8,128)(2,1)} %bitcast.10, f32[1]{0:T(128)S(6)} %copy.15.step_size, f32[1,16]{1,0:T(1,128)} %bitcast.16, f32[1,16]{1,0:T(1,128)} %bitcast.17, ...), custom_call_target="tpu_custom_call" | custom-call | tf_op jit(solution)/shard_map/pallas_call | solution.py:754
  21.7 0.7 %reshape.11 = bf16[4,16,4,256]{3,2,1,0:T(4,128)(2,1)} reshape(bf16[256,256]{1,0:T(8,128)(2,1)S(1)} %shard_map.136) | data formatting | bytes 262144 | tf_op jit(solution)/shard_map/reshape | solution.py:796

commit v5 on v4

--- a/solution.py
+++ b/solution.py
@@ -599,15 +599,18 @@
     ]
     direct = [is_end | up_side, is_end | jnp.logical_not(up_side), is_end]
 
+    marks = [jnp.where(slot < 2, slot, 2 + (slot - 2) * columns) for slot in slots]
+    weights = [jnp.where(slot < 2, 0, 1) for slot in slots]
+
     def sum_copy(n, w):
         return pltpu.make_async_remote_copy(
             send_buf.at[n, w], recv_buf.at[slots[n], w], sum_send.at[0],
-            sum_recv.at[slots[n], w], device_id={"section": targets[n]},
+            sum_recv.at[marks[n] + w * weights[n]], device_id={"section": targets[n]},
         )
 
     def far_copy(w):
         return pltpu.make_async_remote_copy(
-            send_buf.at[far_n, w], recv_buf.at[1, w], sum_send.at[0], sum_recv.at[1, w],
+            send_buf.at[far_n, w], recv_buf.at[1, w], sum_send.at[0], sum_recv.at[1],
             device_id={"section": mirrored(sections - 1)},
         )
 
@@ -621,7 +624,7 @@
 
     def arrived(slot, w):
         pltpu.make_async_copy(
-            recv_buf.at[slot, w], recv_buf.at[slot, w], sum_recv.at[slot, w]
+            recv_buf.at[slot, w], recv_buf.at[slot, w], sum_recv.at[2 + (slot - 2) * columns + w]
         ).wait()
         return recv_buf[slot, w].astype(jnp.float32)
 
@@ -659,18 +662,20 @@
     send(0, (fourth,))
     normalise_next(range(1, columns + 2))
     relay_far(False, 0)
-    for m in range(2):
+    for m in (1, 0):
         hold(1, m * pair_columns, pair_columns)
         send(1, range(m * pair_columns, (m + 1) * pair_columns))
+        if m == 1:
+            relay_far(True, 0)
     relay_far(False, 1)
     normalise_next(range(columns + 2, width - 4))
     relay_far(False, 2)
-    relay_far(True, 0)
+    relay_far(True, 1)
     for m in range(2):
         hold(2, m * pair_columns, pair_columns)
     send(2, range(columns))
     relay_far(False, 3)
-    relay_far(True, 1)
+    relay_far(True, 2)
 
     for m in range(2):
         values = partial(sec, m * pair_columns, pair_columns)
@@ -685,21 +690,24 @@
         for w, own in enumerate(values):
             acc[m * pair_columns + w] = own + conv_bias[...] + residual[w]
 
-    relay_far(True, 2, 3)
+    relay_far(True, 3)
 
     @pl.when(inner)
     def _():
-        for w in range(columns):
+        for w in (2, 3, 0, 1):
             send_buf[2, w] = (held[2, w] + arrived(3, w)).astype(jnp.bfloat16)
             sum_copy(2, w).start()
 
 
-    def finish(order):
-        for n in order[:-1]:
-            for w in range(columns):
-                acc[w] = acc[w] + arrived(n, w)
+    slot_rows = columns * span * half * 2 // 512
+
+    def finish(first, last):
+        wait_rows(slot_rows, sum_recv.at[first])
         for w in range(columns):
-            total = acc[w] + arrived(order[-1], w)
+            acc[w] = acc[w] + recv_buf[first, w].astype(jnp.float32)
+        wait_rows(slot_rows, sum_recv.at[last])
+        for w in range(columns):
+            total = acc[w] + recv_buf[last, w].astype(jnp.float32)
             for c in range(parts):
                 final[c, pl.ds(w, span, stride=columns), :] = total[
                     :, c * channels : (c + 1) * channels
@@ -708,11 +716,11 @@
 
     @pl.when(is_end)
     def _():
-        finish((0, 1))
+        finish(0, 1)
 
     @pl.when(inner)
     def _():
-        finish((1, 0))
+        finish(1, 0)
 
     for n in range(parts):
         out[:, n * channels : (n + 1) * channels] = final[n].astype(out.dtype)
@@ -787,7 +795,7 @@
             dma((1,)),
             dma((1,)),
             dma((1,)),
-            dma((4, columns)),
+            dma((2 + 2 * columns,)),
         ],
         compiler_params=pltpu.CompilerParams(
             collective_id=0, has_side_effects=True, vmem_limit_bytes=40 * 2**20

time: 22.6 us -> 22.1 us (0.978)
  the two profiles are of different devices: /device:TPU:19 before, /device:TPU:0 now
where the time goes in v5:
time: 22.1 us; the launch traced here: 21.8 us
  Pallas kernels  20.5 us (93%)
  local copies, waits for them, and re-layouts  0.69 us (3%)
  between operations  0.66 us (3%)
    pallas_call x1, Pallas kernels, fused_shards(): pl.pallas_call(functools.partial(block_kernel, sizes), out_shape=pltpu.VM...  20.5 us
    reshape x1, local copies, waits for them, and re-layouts, fused_shards(): return out.reshape(frames, height, columns, half)  0.69 us

profile of v5, /device:TPU:0, one launch (start us, length us, event | category | flops | bytes accessed | tf_op | source)
XLA Modules:
  0.0 21.8 jit_solution(8631518299576282127)
XLA Ops:
  0.7 20.5 %shard_map.136 = bf16[256,256]{1,0:T(8,128)(2,1)S(1)} custom-call(f32[2,3072]{1,0:T(2,128)} %modulation_far.1, f32[1,3072]{1,0:T(1,128)} %bitcast.11, f32[1,64]{1,0:T(1,128)} %bitcast.15, bf16[256,16]{1,0:T(8,128)(2,1)} %bitcast.10, f32[1]{0:T(128)S(6)} %copy.15.step_size, f32[1,16]{1,0:T(1,128)} %bitcast.16, f32[1,16]{1,0:T(1,128)} %bitcast.17, ...), custom_call_target="tpu_custom_call" | custom-call | tf_op jit(solution)/shard_map/pallas_call | solution.py:762
  21.2 0.7 %reshape.11 = bf16[4,16,4,256]{3,2,1,0:T(4,128)(2,1)} reshape(bf16[256,256]{1,0:T(8,128)(2,1)S(1)} %shard_map.136) | data formatting | bytes 262144 | tf_op jit(solution)/shard_map/reshape | solution.py:804

commit v6 on v5

--- a/solution.py
+++ b/solution.py
@@ -224,23 +224,6 @@
 
     lead = core == 1
     unit = jnp.where(core >= 0, 1.0, 0.0)
-    barrier = pltpu.get_barrier_semaphore()
-    pl.semaphore_signal(barrier, inc=1, device_id=peer)
-    for k in range(1, sections):
-        pl.semaphore_signal(
-            barrier, inc=1, device_id={"section": lax.rem(sec + k, sections), "tp": 1}
-        )
-
-    @pl.when(has_prev)
-    def _():
-        for k in range(sections):
-            pl.semaphore_signal(
-                barrier,
-                inc=1,
-                device_id={"section": lax.rem(sec + k, sections), "sp": prv, "tp": 1},
-            )
-
-
     groups = (
         ((hidden_far, hidden), (head_far, head_weight)),
         ((modulation_far, modulation), (time_far, time_embed)),
@@ -260,7 +243,27 @@
         [pltpu.make_async_copy(source, target, load_sems.at[n]) for source, target in members]
         for n, members in enumerate(groups)
     ]
-    for c in loads[1] + loads[0] + loads[2]:
+    for c in loads[1] + loads[0]:
+        c.start()
+
+    barrier = pltpu.get_barrier_semaphore()
+    pl.semaphore_signal(barrier, inc=1, device_id=peer)
+    for k in range(1, sections):
+        pl.semaphore_signal(
+            barrier, inc=1, device_id={"section": lax.rem(sec + k, sections), "tp": 1}
+        )
+
+    @pl.when(has_prev)
+    def _():
+        for k in range(sections):
+            pl.semaphore_signal(
+                barrier,
+                inc=1,
+                device_id={"section": lax.rem(sec + k, sections), "sp": prv, "tp": 1},
+            )
+
+
+    for c in loads[2]:
         c.start()
 
     def pair_copy(n, source, target):
@@ -466,6 +469,7 @@
             at_f = ((1 - slot) * frames + f) * folded
             noise_lines[at_f : at_f + folded, :] = jnp.where(lane < lanes, low, high)
 
+    loads[3][0].wait()
     lines_f = jnp.concatenate(
         [
             fields[slot, lax.rem(sec + sections - f, sections), 0]
@@ -511,7 +515,7 @@
     parts = half // channels
     tall = near * height
 
-    def upblock(homes):
+    def upblock(homes, after=None):
         for q in range(2):
             lhs = jnp.concatenate(
                 [
@@ -545,10 +549,12 @@
                 for m, j in enumerate(homes):
                     at_j = pl.ds(pl.multiple_of(2 * j * tall, tall) + q * tall + p, block, stride=2)
                     squares[at_j, :] = total[m * block : (m + 1) * block]
+            if after is not None:
+                for j in homes:
+                    after(2 * j + q)
 
     edge_high = dests[0] > 0
     first_home = jnp.where(edge_high, cols_j - 2, 0)
-    upblock([first_home, first_home + 1])
 
     mine = lax.rem(sec + parts * core, 2 * parts)
     gain = norm_gain[pl.ds(sec, 1), :]
@@ -628,8 +634,7 @@
         ).wait()
         return recv_buf[slot, w].astype(jnp.float32)
 
-    for t in range(4):
-        normalise(2 * first_home + t)
+    upblock([first_home, first_home + 1], normalise)
 
     later = [4, *range(width - 1, width - 2 - columns, -1), *range(5, width - 1 - columns)]
 
@@ -638,7 +643,6 @@
             inward = jnp.where(edge_high, width - 5 - n, 4 + n)
             normalise(jnp.where(is_end, inward, later[n]))
 
-    loads[3][0].wait()
     def hold(n, first_column, count):
         for c, value in enumerate(partial(dests[n], first_column, count)):
             send_buf[n, first_column + c] = value.astype(jnp.bfloat16)

time: 22.1 us -> 22.1 us (level)
  no operation moved by 1% of the time
where the time goes in v6:
time: 22.1 us; the launch traced here: 21.8 us
  Pallas kernels  20.5 us (93%)
  local copies, waits for them, and re-layouts  0.69 us (3%)
  between operations  0.66 us (3%)
    pallas_call x1, Pallas kernels, fused_shards(): pl.pallas_call(functools.partial(block_kernel, sizes), out_shape=pltpu.VM...  20.5 us
    reshape x1, local copies, waits for them, and re-layouts, fused_shards(): return out.reshape(frames, height, columns, half)  0.69 us

profile of v6, /device:TPU:0, one launch (start us, length us, event | category | flops | bytes accessed | tf_op | source)
XLA Modules:
  0.0 21.8 jit_solution(8665227042545717481)
XLA Ops:
  0.7 20.5 %shard_map.136 = bf16[256,256]{1,0:T(8,128)(2,1)S(1)} custom-call(f32[2,3072]{1,0:T(2,128)} %modulation_far.1, f32[1,3072]{1,0:T(1,128)} %bitcast.11, f32[1,64]{1,0:T(1,128)} %bitcast.15, bf16[256,16]{1,0:T(8,128)(2,1)} %bitcast.10, f32[1]{0:T(128)S(6)} %copy.15.step_size, f32[1,16]{1,0:T(1,128)} %bitcast.16, f32[1,16]{1,0:T(1,128)} %bitcast.17, ...), custom_call_target="tpu_custom_call" | custom-call | tf_op jit(solution)/shard_map/pallas_call | solution.py:766
  21.1 0.7 %reshape.11 = bf16[4,16,4,256]{3,2,1,0:T(4,128)(2,1)} reshape(bf16[256,256]{1,0:T(8,128)(2,1)S(1)} %shard_map.136) | data formatting | bytes 262144 | tf_op jit(solution)/shard_map/reshape | solution.py:808

commit v7 on v6

--- a/solution.py
+++ b/solution.py
@@ -293,13 +293,16 @@
 
     def spread():
         for z in [*others, sec]:
-            for c in (0, 1):
-                if z is not sec:
-                    spread_copy(z, 0, c).start()
-
-                @pl.when(has_next)
-                def _():
+            if z is not sec:
+                spread_copy(z, 0, 0).start()
+
+            @pl.when(has_next)
+            def _():
+                for c in (0, 1):
                     spread_copy(z, 1, c).start()
+
+            if z is not sec:
+                spread_copy(z, 0, 1).start()
 
         pltpu.make_async_remote_copy(
             fields.at[0, 0], fields.at[0, 0], field_send.at[0], field_recv.at[0], device_id=peer

time: 22.1 us -> 22 us (level)
  no operation moved by 1% of the time
where the time goes in v7:
time: 22 us; the launch traced here: 21.8 us
  Pallas kernels  20.5 us (93%)
  local copies, waits for them, and re-layouts  0.69 us (3%)
  between operations  0.66 us (3%)
    pallas_call x1, Pallas kernels, fused_shards(): pl.pallas_call(functools.partial(block_kernel, sizes), out_shape=pltpu.VM...  20.5 us
    reshape x1, local copies, waits for them, and re-layouts, fused_shards(): return out.reshape(frames, height, columns, half)  0.69 us

profile of v7, /device:TPU:0, one launch (start us, length us, event | category | flops | bytes accessed | tf_op | source)
XLA Modules:
  0.0 21.8 jit_solution(14677777099250137443)
XLA Ops:
  0.7 20.5 %shard_map.136 = bf16[256,256]{1,0:T(8,128)(2,1)S(1)} custom-call(f32[2,3072]{1,0:T(2,128)} %modulation_far.1, f32[1,3072]{1,0:T(1,128)} %bitcast.11, f32[1,64]{1,0:T(1,128)} %bitcast.15, bf16[256,16]{1,0:T(8,128)(2,1)} %bitcast.10, f32[1]{0:T(128)S(6)} %copy.15.step_size, f32[1,16]{1,0:T(1,128)} %bitcast.16, f32[1,16]{1,0:T(1,128)} %bitcast.17, ...), custom_call_target="tpu_custom_call" | custom-call | tf_op jit(solution)/shard_map/pallas_call | solution.py:769
  21.2 0.7 %reshape.11 = bf16[4,16,4,256]{3,2,1,0:T(4,128)(2,1)} reshape(bf16[256,256]{1,0:T(8,128)(2,1)S(1)} %shard_map.136) | data formatting | bytes 262144 | tf_op jit(solution)/shard_map/reshape | solution.py:811
